TPU v7x, 256 devices: a whole 4x4x8 slice. The times are simulated.
256 devices in a mesh: sy: 16 (over y, z_lo), sx: 16 (over z_hi, x, core).
Axes of the slice: x: 4, y: 4, z: 8 (z_hi: 2, z_lo: 4; z = z_hi * 4 + z_lo), core: 2. Of those that a mesh axis runs over, the one named last changes fastest.
Arguments:
- object_re: float32 [4096, 4096], P('sy', 'sx'), may hold values from -6 to 6
- object_im: float32 [4096, 4096], P('sy', 'sx'), may hold values from -6 to 6
- probe_re: float32 [2, 256, 256], replicated, may hold values from -6 to 6
- probe_im: float32 [2, 256, 256], replicated, may hold values from -6 to 6
- amplitudes: float32 [16, 16, 8, 256, 256], P('sy', 'sx'), may hold values from 0.5 to 3
- offsets: int32 [16, 16, 8, 2], P('sy', 'sx'), may hold values from -128 to 127
- visit_order: int32 [16, 16, 8], P('sy', 'sx'), may hold values from 0 to 7, each once within a row
Outputs:
- object_new_re: float32 [4096, 4096], P('sy', 'sx')
- object_new_im: float32 [4096, 4096], P('sy', 'sx')
- probe_new_re: float32 [2, 256, 256], replicated
- probe_new_im: float32 [2, 256, 256], replicated
Inputs may be any that keep to these rules, and one draw needn't show every extreme that they name: `visit_order`: each tile's entries are a permutation of 0 to 7.
All inputs are finite; a program needn't handle non-finite values.
Results may differ from a plain program's by a relative error of at most 0.0019.
Values sent between devices are 32-bit elements; how exact they have to be, the bound alone decides.
A program may use at most 64 MiB of HBM per device.

v0:
```python
import functools
import math

import numpy as np

import jax
import jax.numpy as jnp
from jax import lax
from jax.experimental import pallas as pl
from jax.experimental.pallas import tpu as pltpu
from jax.sharding import PartitionSpec as P

MESH = pl.DeviceIdType.MESH
BATCHES = 2
OBJECT_RATE = 0.25
PROBE_GAIN = 4.0
F = 256
H = 128
E = F + 2 * H
ROWS = 16
COLS = 16
VMEM = pl.BlockSpec(memory_space=pltpu.VMEM)
SMEM = pl.BlockSpec(memory_space=pltpu.SMEM)
ANY = pl.BlockSpec(memory_space=pl.ANY)
DIRECTIONS = [(dr, dc) for dr in (-1, 0, 1) for dc in (-1, 0, 1) if (dr, dc) != (0, 0)]
TILE_ROWS = {-1: (H, H), 0: (H, F), 1: (F, H)}
TILE_PLANES = {-1: (1, 1), 0: (1, 2), 1: (2, 1)}
OUTER_ROWS = {-1: (0, H), 0: (H, F), 1: (H + F, H)}
OUTER_PLANES = {-1: (0, 1), 0: (1, 2), 1: (3, 1)}
FRAME_ROWS = {-1: (H + F, H), 0: (H, F), 1: (0, H)}
FRAME_PLANES = {-1: (3, 1), 0: (1, 2), 1: (0, 1)}
INNER_ROWS = {-1: (F, H), 0: (H, F), 1: (H, H)}
INNER_PLANES = {-1: (2, 1), 0: (1, 2), 1: (1, 1)}


def table(frame_size):
    ramp = np.arange(frame_size, dtype=np.int64)
    product = (ramp[:, None] * ramp[None, :]) % frame_size
    angle = np.float32(2.0 * math.pi / frame_size) * product.astype(np.float32)
    scale = np.float32(1.0 / math.sqrt(frame_size))
    return np.cos(angle) * scale, -np.sin(angle) * scale


def dft_operands():
    re, im = table(F)
    left = np.block([[re, -im], [im, re]])
    back_left = np.block([[re, im], [-im, re]])
    right = np.block([[re, im], [-im, re]])
    back_right = np.block([[re, -im], [im, re]])
    return [jnp.asarray(m, jnp.float32).astype(jnp.bfloat16) for m in (left, back_left, right, back_right)]


def part(pair):
    return pl.ds(pair[0], pair[1])


def inside(row, col):
    return (row >= 0) & (row < ROWS) & (col >= 0) & (col < COLS)


def greet_neighbours(row, col):
    barrier = pltpu.get_barrier_semaphore()
    count = jnp.int32(0)
    for dr, dc in DIRECTIONS:
        there = inside(row + dr, col + dc)

        @pl.when(there)
        def _():
            pl.semaphore_signal(barrier, inc=1, device_id=(row + dr, col + dc), device_id_type=MESH)

        count = count + there.astype(jnp.int32)
    pl.semaphore_wait(barrier, count)


def exchange(row, col, make):
    for k, (dr, dc) in enumerate(DIRECTIONS):

        @pl.when(inside(row + dr, col + dc))
        def _():
            for copy in make(k, dr, dc, (row + dr, col + dc)):
                copy.start()


def finish(row, col, make):
    for k, (dr, dc) in enumerate(DIRECTIONS):

        @pl.when(inside(row - dr, col - dc))
        def _():
            for copy in make(k, dr, dc, (row - dr, col - dc)):
                copy.wait_recv()

    for k, (dr, dc) in enumerate(DIRECTIONS):

        @pl.when(inside(row + dr, col + dc))
        def _():
            for copy in make(k, dr, dc, (row + dr, col + dc)):
                copy.wait_send()


def clear_edges(row, col, frame):
    @pl.when(row == 0)
    def _():
        frame[:, :, 0:H, :] = jnp.zeros((2, 4, H, H), jnp.float32)

    @pl.when(row == ROWS - 1)
    def _():
        frame[:, :, H + F : E, :] = jnp.zeros((2, 4, H, H), jnp.float32)

    @pl.when(col == 0)
    def _():
        frame[:, 0] = jnp.zeros((2, E, H), jnp.float32)

    @pl.when(col == COLS - 1)
    def _():
        frame[:, 3] = jnp.zeros((2, E, H), jnp.float32)


def halo_kernel(re_ref, im_ref, frame, send_sem, recv_sem):
    row, col = lax.axis_index("sy"), lax.axis_index("sx")
    greet_neighbours(row, col)

    def make(k, dr, dc, device):
        rows, count = TILE_ROWS[dr]
        plane, planes = TILE_PLANES[dc]
        return [
            pltpu.make_async_remote_copy(
                src_ref=source.at[pl.ds(rows - H, count), pl.ds((plane - 1 + n) * H, H)],
                dst_ref=frame.at[channel, FRAME_PLANES[dc][0] + n, part(FRAME_ROWS[dr])],
                send_sem=send_sem.at[channel, n, k],
                recv_sem=recv_sem.at[channel, n, k],
                device_id=device,
                device_id_type=MESH,
            )
            for channel, source in enumerate((re_ref, im_ref))
            for n in range(planes)
        ]

    exchange(row, col, make)
    clear_edges(row, col, frame)
    for channel, source in enumerate((re_ref, im_ref)):
        for n in range(2):
            frame[channel, 1 + n, H : H + F] = source[:, n * H : (n + 1) * H]
    finish(row, col, make)


def fold_into(row, col, accum, bufs, send_sem, recv_sem, begin, add):
    def make(k, dr, dc, device):
        return [
            pltpu.make_async_remote_copy(
                src_ref=accum.at[:, part(OUTER_PLANES[dc]), part(OUTER_ROWS[dr])],
                dst_ref=bufs[k],
                send_sem=send_sem.at[k],
                recv_sem=recv_sem.at[k],
                device_id=device,
                device_id_type=MESH,
            )
        ]

    exchange(row, col, make)
    begin()
    finish(row, col, make)
    for k, (dr, dc) in enumerate(DIRECTIONS):

        @pl.when(inside(row - dr, col - dc))
        def _():
            add(k, INNER_ROWS[dr], INNER_PLANES[dc])


def mid_kernel(accum, old, frame, b0, b1, b2, b3, b4, b5, b6, b7, send_sem, recv_sem, send2, recv2):
    row, col = lax.axis_index("sy"), lax.axis_index("sx")
    greet_neighbours(row, col)
    bufs = (b0, b1, b2, b3, b4, b5, b6, b7)

    def begin():
        clear_edges(row, col, frame)
        frame[:, 1:3, H : H + F] = old[:, 1:3, H : H + F] + accum[:, 1:3, H : H + F]

    def add(k, rows, planes):
        where = (slice(None), part(planes), part(rows))
        frame[where] = frame[where] + bufs[k][...]

    fold_into(row, col, accum, bufs, send_sem, recv_sem, begin, add)

    def make(k, dr, dc, device):
        return [
            pltpu.make_async_remote_copy(
                src_ref=frame.at[:, part(TILE_PLANES[dc]), part(TILE_ROWS[dr])],
                dst_ref=frame.at[:, part(FRAME_PLANES[dc]), part(FRAME_ROWS[dr])],
                send_sem=send2.at[k],
                recv_sem=recv2.at[k],
                device_id=device,
                device_id_type=MESH,
            )
        ]

    exchange(row, col, make)
    finish(row, col, make)


def fold_kernel(accum, old, out_re, out_im, b0, b1, b2, b3, b4, b5, b6, b7, send_sem, recv_sem):
    row, col = lax.axis_index("sy"), lax.axis_index("sx")
    greet_neighbours(row, col)
    bufs = (b0, b1, b2, b3, b4, b5, b6, b7)
    outs = (out_re, out_im)

    def begin():
        for channel, out in enumerate(outs):
            for n in range(2):
                out[:, n * H : (n + 1) * H] = old[channel, 1 + n, H : H + F] + accum[channel, 1 + n, H : H + F]

    def add(k, rows, planes):
        for channel, out in enumerate(outs):
            for n in range(planes[1]):
                where = (pl.ds(rows[0] - H, rows[1]), pl.ds((planes[0] - 1 + n) * H, H))
                out[where] = out[where] + bufs[k][channel, n]

    fold_into(row, col, accum, bufs, send_sem, recv_sem, begin, add)


def strip_buffers():
    return [
        pltpu.VMEM((2, OUTER_PLANES[dc][1], OUTER_ROWS[dr][1], H), jnp.float32) for dr, dc in DIRECTIONS
    ]


CHUNK1 = 64
CHUNK2 = 16
COLORS = (("x", "y"), ("y", "x"))


def sum_kernel(g, probe, out, r0, w0, r1, w1, r2, w2, r3, w4, s0, q0, s1, q1, s2, q2, s3, q3, s4, q4, s5, q5, s6, q6):
    sy, sx = lax.axis_index("sy"), lax.axis_index("sx")
    here = {
        "y": lax.div(sy, 4),
        "x": lax.div(lax.rem(sx, 8), 2),
        "z": lax.div(sx, 8) * 4 + lax.rem(sy, 4),
        "core": lax.rem(sx, 2),
    }
    size = {"x": 4, "y": 4, "z": 8, "core": 2}
    rate = PROBE_GAIN / (8 * math.sqrt(ROWS * COLS))

    def place(axis, step):
        there = dict(here)
        there[axis] = lax.rem(here[axis] + step, size[axis])
        device = (
            there["y"] * 4 + lax.rem(there["z"], 4),
            lax.div(there["z"], 4) * 8 + there["x"] * 2 + there["core"],
        )
        return there[axis], device

    def send(src, dst, ss, rs, device):
        copy = pltpu.make_async_remote_copy(
            src_ref=src, dst_ref=dst, send_sem=ss, recv_sem=rs, device_id=device, device_id_type=MESH
        )
        copy.start()
        return copy

    barrier = pltpu.get_barrier_semaphore()
    for axis in ("core", "x", "y", "z"):
        for step in range(1, size[axis]):
            pl.semaphore_signal(barrier, inc=1, device_id=place(axis, step)[1], device_id_type=MESH)
    pl.semaphore_wait(barrier, 1 + 3 + 3 + 7)

    core = here["core"]
    other, partner = place("core", 1)
    mine = pl.ds(pl.multiple_of(core * 512, 512), 512)
    theirs = pl.ds(pl.multiple_of(other * 512, 512), 512)
    send(g.at[theirs], r0, s0, q0, partner).wait()
    w0[...] = g[mine] + r0[...]

    copies = []
    for c, (first, second) in enumerate(COLORS):
        for step in (1, 2, 3):
            index, device = place(first, step)
            source = w0.at[pl.ds(pl.multiple_of(c * 256 + index * CHUNK1, CHUNK1), CHUNK1)]
            copies.append(send(source, r1.at[c, step - 1], s1.at[c, step - 1], q1.at[c, step - 1], device))
    for copy in copies:
        copy.wait()
    for c, (first, second) in enumerate(COLORS):
        own = w0[pl.ds(pl.multiple_of(c * 256 + here[first] * CHUNK1, CHUNK1), CHUNK1)]
        w1[c] = (own + r1[c, 0]) + (r1[c, 1] + r1[c, 2])

    copies = []
    for c, (first, second) in enumerate(COLORS):
        for step in (1, 2, 3):
            index, device = place(second, step)
            source = w1.at[c, pl.ds(pl.multiple_of(index * CHUNK2, CHUNK2), CHUNK2)]
            copies.append(send(source, r2.at[c, step - 1], s2.at[c, step - 1], q2.at[c, step - 1], device))
    for copy in copies:
        copy.wait()
    for c, (first, second) in enumerate(COLORS):
        own = w1[c, pl.ds(pl.multiple_of(here[second] * CHUNK2, CHUNK2), CHUNK2)]
        w2[c] = (own + r2[c, 0]) + (r2[c, 1] + r2[c, 2])

    copies = []
    for c in range(2):
        for step in range(1, 8):
            index, device = place("z", step)
            copies.append(send(w2.at[c], r3.at[c, here["z"]], s3.at[c, step - 1], q3.at[c, step - 1], device))
    for c in range(2):
        r3[c, here["z"]] = w2[c]
    for copy in copies:
        copy.wait()
    for c, (first, second) in enumerate(COLORS):
        total = ((r3[c, 0] + r3[c, 1]) + (r3[c, 2] + r3[c, 3])) + ((r3[c, 4] + r3[c, 5]) + (r3[c, 6] + r3[c, 7]))
        start = core * 512 + c * 256 + here[first] * CHUNK1 + here[second] * CHUNK2
        base = probe[pl.ds(pl.multiple_of(start, CHUNK2), CHUNK2)]
        w4[c, pl.ds(pl.multiple_of(here[second] * CHUNK2, CHUNK2), CHUNK2)] = base + rate * total

    copies = []
    for c, (first, second) in enumerate(COLORS):
        spot = w4.at[c, pl.ds(pl.multiple_of(here[second] * CHUNK2, CHUNK2), CHUNK2)]
        for step in (1, 2, 3):
            copies.append(send(spot, spot, s4.at[c, step - 1], q4.at[c, step - 1], place(second, step)[1]))
    for copy in copies:
        copy.wait()

    copies = []
    for c, (first, second) in enumerate(COLORS):
        start = core * 512 + c * 256 + here[first] * CHUNK1
        spot = out.at[pl.ds(pl.multiple_of(start, CHUNK1), CHUNK1)]
        for step in (1, 2, 3):
            copies.append(send(w4.at[c], spot, s5.at[c, step - 1], q5.at[c, step - 1], place(first, step)[1]))
    for c, (first, second) in enumerate(COLORS):
        start = core * 512 + c * 256 + here[first] * CHUNK1
        out[pl.ds(pl.multiple_of(start, CHUNK1), CHUNK1)] = w4[c]
    for copy in copies:
        copy.wait()

    send(out.at[mine], out.at[mine], s6, q6, partner).wait()


def work_kernel(batch, order, offsets, frame, probe_re, probe_im, amps, left, back_left, right, back_right, *rest):
    if batch == 0:
        accum, grad, patch, fields, halves, amp, amp_sem = rest
        grad_in = None
    else:
        grad_in, accum, grad, patch, fields, halves, amp, amp_sem = rest
    size = 4
    loads = []
    for j in range(size):
        p = order[batch * size + j]
        load = pltpu.make_async_copy(amps.at[p], amp.at[j], amp_sem.at[j])
        load.start()
        loads.append(load)

    power = jnp.max(
        probe_re[0] * probe_re[0]
        + probe_im[0] * probe_im[0]
        + (probe_re[1] * probe_re[1] + probe_im[1] * probe_im[1])
    )
    scale = OBJECT_RATE / jnp.full((8, 128), power, jnp.float32)[0:1, 0:1]
    accum[...] = jnp.zeros_like(accum)
    for j in range(size):
        p = order[batch * size + j]
        top = offsets[p, 0] + H
        shift = offsets[p, 1] + H
        for ch in range(2):
            rows = jnp.concatenate([frame[ch, n, pl.ds(top, F), :] for n in range(4)], axis=1)
            patch[j, ch] = pltpu.roll(rows, lax.rem(E - shift, E), 1)[:, :F]
        re, im = patch[j, 0], patch[j, 1]
        for m in range(2):
            at = pl.ds((2 * j + m) * F, F)
            fields[0:F, at] = (probe_re[m] * re - probe_im[m] * im).astype(jnp.bfloat16)
            fields[F : 2 * F, at] = (probe_re[m] * im + probe_im[m] * re).astype(jnp.bfloat16)
    for n in range(2 * size):
        half = jnp.dot(left[...], fields[0 : 2 * F, n * F : (n + 1) * F], preferred_element_type=jnp.float32)
        halves[n * F : (n + 1) * F, 0:F] = half[0:F].astype(jnp.bfloat16)
        halves[n * F : (n + 1) * F, F : 2 * F] = half[F:].astype(jnp.bfloat16)
    for j in range(size):
        far = jnp.dot(halves[2 * j * F : 2 * (j + 1) * F, :], right[...], preferred_element_type=jnp.float32)
        squares = far * far
        intensity = (squares[0:F, 0:F] + squares[0:F, F:]) + (squares[F:, 0:F] + squares[F:, F:])
        loads[j].wait()
        ratio = amp[j] * lax.rsqrt(jnp.maximum(intensity, 1.0))
        for m in range(2):
            at = (2 * j + m) * F
            fields[2 * F : 3 * F, at : at + F] = (far[m * F : (m + 1) * F, 0:F] * ratio).astype(jnp.bfloat16)
            fields[3 * F : 4 * F, at : at + F] = (far[m * F : (m + 1) * F, F:] * ratio).astype(jnp.bfloat16)
    for n in range(2 * size):
        half = jnp.dot(back_left[...], fields[2 * F :, n * F : (n + 1) * F], preferred_element_type=jnp.float32)
        halves[n * F : (n + 1) * F, 0:F] = half[0:F].astype(jnp.bfloat16)
        halves[n * F : (n + 1) * F, F : 2 * F] = half[F:].astype(jnp.bfloat16)
    for j in range(size):
        p = order[batch * size + j]
        top = offsets[p, 0] + H
        shift = offsets[p, 1] + H
        back = jnp.dot(halves[2 * j * F : 2 * (j + 1) * F, :], back_right[...], preferred_element_type=jnp.float32)
        re, im = patch[j, 0], patch[j, 1]
        terms = [None, None]
        for m in range(2):
            at = (2 * j + m) * F
            d_re = back[m * F : (m + 1) * F, 0:F] - fields[0:F, at : at + F].astype(jnp.float32)
            d_im = back[m * F : (m + 1) * F, F:] - fields[F : 2 * F, at : at + F].astype(jnp.float32)
            o_re = probe_re[m] * d_re + probe_im[m] * d_im
            o_im = probe_re[m] * d_im - probe_im[m] * d_re
            g_re = re * d_re + im * d_im
            g_im = re * d_im - im * d_re
            if m == 0:
                terms = [o_re, o_im]
            else:
                terms = [terms[0] + o_re, terms[1] + o_im]
            for ch, g in enumerate((g_re, g_im)):
                if j == 0:
                    grad[ch, m] = g if grad_in is None else grad_in[ch, m] + g
                else:
                    grad[ch, m] = grad[ch, m] + g
        for ch in range(2):
            wide = jnp.concatenate([terms[ch] * scale, jnp.zeros((F, F), jnp.float32)], axis=1)
            wide = pltpu.roll(wide, shift, 1)
            for n in range(4):
                accum[ch, n, pl.ds(top, F), :] += wide[:, n * H : (n + 1) * H]


def local(object_re, object_im, probe_re, probe_im, amplitudes, offsets, visit_order):
    f32 = jnp.float32
    amps = amplitudes.reshape(8, F, F)
    offs = offsets.reshape(8, 2)
    order = visit_order.reshape(8)
    tables = dft_operands()
    frame_shape = jax.ShapeDtypeStruct((2, 4, E, H), f32)
    grad_shape = jax.ShapeDtypeStruct((2, 2, F, F), f32)
    limit = 60 * 1024 * 1024

    def comm(kernel, outs, scratch, ident, n_in):
        return pl.pallas_call(
            kernel,
            out_shape=outs,
            in_specs=[VMEM] * n_in,
            out_specs=[VMEM] * len(outs) if isinstance(outs, list) else VMEM,
            scratch_shapes=scratch,
            compiler_params=pltpu.CompilerParams(
                collective_id=ident, has_side_effects=True, vmem_limit_bytes=limit
            ),
        )

    dma = pltpu.SemaphoreType.DMA

    def work(batch, frame, grad):
        ins = [order, offs, frame, probe_re, probe_im, amps, *tables]
        specs = [SMEM, SMEM, VMEM, VMEM, VMEM, ANY] + [VMEM] * 4
        if grad is not None:
            ins.append(grad)
            specs.append(VMEM)
        return pl.pallas_call(
            functools.partial(work_kernel, batch),
            out_shape=[frame_shape, grad_shape],
            in_specs=specs,
            out_specs=[VMEM, VMEM],
            scratch_shapes=[
                pltpu.VMEM((4, 2, F, F), f32),
                pltpu.VMEM((4 * F, 8 * F), jnp.bfloat16),
                pltpu.VMEM((8 * F, 2 * F), jnp.bfloat16),
                pltpu.VMEM((4, F, F), f32),
                dma((4,)),
            ],
            compiler_params=pltpu.CompilerParams(vmem_limit_bytes=limit),
            cost_estimate=pl.CostEstimate(flops=4_300_000_000, bytes_accessed=10_000_000, transcendentals=262144),
        )(*ins)

    frame = comm(halo_kernel, frame_shape, [dma((2, 2, 8)), dma((2, 2, 8))], 0, 2)(object_re, object_im)
    accum, grad = work(0, frame, None)
    frame = comm(
        mid_kernel, frame_shape, strip_buffers() + [dma((8,))] * 4, 1, 2
    )(accum, frame)
    accum, grad = work(1, frame, grad)
    out = comm(
        fold_kernel, [jax.ShapeDtypeStruct((F, F), f32)] * 2, strip_buffers() + [dma((8,))] * 2, 2, 2
    )(accum, frame)
    probe = jnp.stack([probe_re, probe_im])
    flat = comm(
        sum_kernel,
        jax.ShapeDtypeStruct((1024, F), f32),
        [
            pltpu.VMEM((512, F), f32),
            pltpu.VMEM((512, F), f32),
            pltpu.VMEM((2, 3, CHUNK1, F), f32),
            pltpu.VMEM((2, CHUNK1, F), f32),
            pltpu.VMEM((2, 3, CHUNK2, F), f32),
            pltpu.VMEM((2, CHUNK2, F), f32),
            pltpu.VMEM((2, 8, CHUNK2, F), f32),
            pltpu.VMEM((2, CHUNK1, F), f32),
            dma, dma,
            dma((2, 3)), dma((2, 3)),
            dma((2, 3)), dma((2, 3)),
            dma((2, 7)), dma((2, 7)),
            dma((2, 3)), dma((2, 3)),
            dma((2, 3)), dma((2, 3)),
            dma, dma,
        ],
        3,
        2,
    )(grad.reshape(1024, F), probe.reshape(1024, F))
    new = flat.reshape(2, 2, F, F)
    return (out[0], out[1], new[0], new[1])


def solution(mesh):
    return jax.shard_map(
        local,
        mesh=mesh,
        in_specs=(
            P("sy", "sx"),
            P("sy", "sx"),
            P(),
            P(),
            P("sy", "sx", None, None, None),
            P("sy", "sx", None, None),
            P("sy", "sx", None),
        ),
        out_specs=(P("sy", "sx"), P("sy", "sx"), P(), P()),
        check_vma=False,
    )
```

profile of v0, /device:TPU:1, one launch (start us, length us, event | category | flops | bytes accessed | tf_op | source)
XLA Modules:
  0.0 214.6 jit_solution(10520197562342979316)
XLA Ops:
  0.6 0.0 copy-start.4
  0.6 18.1 %shard_map.138.frame.old = f32[2,4,512,128]{3,2,1,0:T(8,128)} custom-call(f32[256,256]{1,0:T(8,128)} %re_ref.1, f32[256,256]{1,0:T(8,128)} %im_ref.1), custom_call_target="tpu_custom_call" | custom-call | tf_op jit(solution)/shard_map/pallas_call | solution.py:461
  18.7 0.0 copy-done.4
  18.7 0.7 copy.16.offsets
  19.4 11.5 %shard_map.139 = (f32[2,4,512,128]{3,2,1,0:T(8,128)}, f32[2,2,256,256]{3,2,1,0:T(8,128)}) custom-call(s32[8]{0:T(128)} %bitcast.18, s32[8,2]{1,0:T(8,128)} %copy.16.offsets, f32[2,4,512,128]{3,2,1,0:T(8,128)} %shard_map.138.frame.old, f32[2,256,256]{2,1,0:T(8,128)} %probe_re.3, f32[2,256,256]{2,1,0:T(8,128)} %probe_im.3, f32[8,256,256]{2,1,0:T(8,128)} %bitcast.16, ...), custom_call_target="tpu_custom_call" | custom-call | flops 4300000256 | bytes 10000000 | tf_op jit(solution)/shard_map/pallas_call | solution.py:445
  31.0 42.8 %shard_map.140.frame.old = f32[2,4,512,128]{3,2,1,0:T(8,128)} custom-call(f32[2,4,512,128]{3,2,1,0:T(8,128)} %get-tuple-element.10.accum, f32[2,4,512,128]{3,2,1,0:T(8,128)} %shard_map.138.frame.old), custom_call_target="tpu_custom_call" | custom-call | tf_op jit(solution)/shard_map/pallas_call | solution.py:463
  73.7 11.8 %shard_map.141 = (f32[2,4,512,128]{3,2,1,0:T(8,128)}, f32[2,2,256,256]{3,2,1,0:T(8,128)}) custom-call(s32[8]{0:T(128)} %bitcast.19, s32[8,2]{1,0:T(8,128)} %copy.16.offsets, f32[2,4,512,128]{3,2,1,0:T(8,128)} %shard_map.140.frame.old, f32[2,256,256]{2,1,0:T(8,128)} %probe_re.3, f32[2,256,256]{2,1,0:T(8,128)} %probe_im.3, f32[8,256,256]{2,1,0:T(8,128)} %bitcast.17, ...), custom_call_target="tpu_custom_call" | custom-call | flops 4300000256 | bytes 10000000 | tf_op jit(solution)/shard_map/pallas_call | solution.py:445
  85.5 0.0 copy-start
  85.5 0.0 copy-start.1
  85.5 35.8 %shard_map.142 = (f32[256,256]{1,0:T(8,128)}, f32[256,256]{1,0:T(8,128)}) custom-call(f32[2,4,512,128]{3,2,1,0:T(8,128)} %get-tuple-element.12.accum, f32[2,4,512,128]{3,2,1,0:T(8,128)} %shard_map.140.frame.old), custom_call_target="tpu_custom_call" | custom-call | tf_op jit(solution)/shard_map/pallas_call | solution.py:467
  121.4 0.0 copy-done
  121.4 0.0 copy-done.1
  121.4 1.0 pad_maximum_fusion
  122.4 0.0 copy-start.3
  122.4 88.4 %shard_map.143 = f32[1024,256]{1,0:T(8,128)} custom-call(f32[1024,256]{1,0:T(8,128)} %bitcast.10, f32[1024,256]{1,0:T(8,128)} %bitcast.9), custom_call_target="tpu_custom_call" | custom-call | tf_op jit(solution)/shard_map/pallas_call | solution.py:471
  210.9 0.0 copy-start.2
  210.9 2.3 %fusion = (f32[512,256]{1,0:T(8,128)}, f32[512,256]{1,0:T(8,128)}) fusion(f32[1024,256]{1,0:T(8,128)} %shard_map.143), kind=kLoop, calls=%fused_computation.1 | loop fusion | bytes 2097152 | tf_op jit(solution)/shard_map/slice | solution.py:495
  213.2 0.0 copy-done.3
  213.2 0.7 copy.19
  213.9 0.0 copy-done.2
  213.9 0.7 copy.20
Async XLA Ops:
  0.6 18.1 %copy-start.4 = (s32[1,1,8,2]{2,3,1,0:T(2,128)S(1)}, s32[1,1,8,2]{2,3,1,0:T(2,128)}, u32[]{:S(2)}) copy-start(s32[1,1,8,2]{2,3,1,0:T(2,128)} %param.16) | copy-start | bytes 196
  85.5 35.9 %copy-start = (f32[2,256,256]{2,1,0:T(8,128)S(1)}, f32[2,256,256]{2,1,0:T(8,128)}, u32[]{:S(2)}) copy-start(f32[2,256,256]{2,1,0:T(8,128)} %probe_re.3) | copy-start | bytes 1572868
  85.5 35.9 %copy-start.1 = (f32[2,256,256]{2,1,0:T(8,128)S(1)}, f32[2,256,256]{2,1,0:T(8,128)}, u32[]{:S(2)}) copy-start(f32[2,256,256]{2,1,0:T(8,128)} %probe_im.3) | copy-start | bytes 1572868
  122.4 90.7 %copy-start.3 = (f32[256,256]{1,0:T(8,128)S(1)}, f32[256,256]{1,0:T(8,128)}, u32[]{:S(2)}) copy-start(f32[256,256]{1,0:T(8,128)} %get-tuple-element.22) | copy-start | bytes 786436
  210.9 3.0 %copy-start.2 = (f32[256,256]{1,0:T(8,128)S(1)}, f32[256,256]{1,0:T(8,128)}, u32[]{:S(2)}) copy-start(f32[256,256]{1,0:T(8,128)} %get-tuple-element.23) | copy-start | bytes 786436
where the time goes:
time: 215 us
  Pallas kernels  208 us (97%)
  local copies, waits for them, and re-layouts  4.38 us (2%)
    pallas_call x1, Pallas kernels, local(): comm(sum_kernel, jax.ShapeDtypeStruct((1024, F), f32), [pltpu.VMEM((512,...  88.4 us
    pallas_call x1, Pallas kernels, local(): comm(mid_kernel, frame_shape, strip_buffers() + [dma((8,))] * 4, 1, 2)  42.8 us
    pallas_call x1, Pallas kernels, local(): comm(fold_kernel, [jax.ShapeDtypeStruct((F, F), f32)] * 2, strip_buffers(...  35.8 us
    pallas_call x2, Pallas kernels, work(): pl.pallas_call(functools.partial(work_kernel, batch), out_shape=[frame_sh...  23.3 us
    pallas_call x1, Pallas kernels, local(): comm(halo_kernel, frame_shape, [dma((2, 2, 8)), dma((2, 2, 8))], 0, 2)  18.1 us

commit v1 on v0

--- a/solution.py
+++ b/solution.py
@@ -19,10 +19,10 @@
 E = F + 2 * H
 ROWS = 16
 COLS = 16
+SEAM = 8
 VMEM = pl.BlockSpec(memory_space=pltpu.VMEM)
 SMEM = pl.BlockSpec(memory_space=pltpu.SMEM)
 ANY = pl.BlockSpec(memory_space=pl.ANY)
-DIRECTIONS = [(dr, dc) for dr in (-1, 0, 1) for dc in (-1, 0, 1) if (dr, dc) != (0, 0)]
 TILE_ROWS = {-1: (H, H), 0: (H, F), 1: (F, H)}
 TILE_PLANES = {-1: (1, 1), 0: (1, 2), 1: (2, 1)}
 OUTER_ROWS = {-1: (0, H), 0: (H, F), 1: (H + F, H)}
@@ -58,43 +58,78 @@
     return (row >= 0) & (row < ROWS) & (col >= 0) & (col < COLS)
 
 
-def greet_neighbours(row, col):
+def greet(peers):
     barrier = pltpu.get_barrier_semaphore()
     count = jnp.int32(0)
-    for dr, dc in DIRECTIONS:
-        there = inside(row + dr, col + dc)
+    for there, device in peers:
 
         @pl.when(there)
         def _():
-            pl.semaphore_signal(barrier, inc=1, device_id=(row + dr, col + dc), device_id_type=MESH)
+            pl.semaphore_signal(barrier, inc=1, device_id=device, device_id_type=MESH)
 
         count = count + there.astype(jnp.int32)
     pl.semaphore_wait(barrier, count)
 
 
-def exchange(row, col, make):
-    for k, (dr, dc) in enumerate(DIRECTIONS):
-
-        @pl.when(inside(row + dr, col + dc))
-        def _():
-            for copy in make(k, dr, dc, (row + dr, col + dc)):
-                copy.start()
-
-
-def finish(row, col, make):
-    for k, (dr, dc) in enumerate(DIRECTIONS):
-
-        @pl.when(inside(row - dr, col - dc))
-        def _():
-            for copy in make(k, dr, dc, (row - dr, col - dc)):
-                copy.wait_recv()
-
-    for k, (dr, dc) in enumerate(DIRECTIONS):
-
-        @pl.when(inside(row + dr, col + dc))
-        def _():
-            for copy in make(k, dr, dc, (row + dr, col + dc)):
-                copy.wait_send()
+class Spot:
+    def __init__(self):
+        self.row, self.col = lax.axis_index("sy"), lax.axis_index("sx")
+
+    def at(self, dr, dc):
+        return (self.row + dr, self.col + dc)
+
+    def has(self, dr, dc):
+        return inside(self.row + dr, self.col + dc)
+
+    def far(self, dc):
+        return self.col == (SEAM - 1 if dc > 0 else SEAM)
+
+    def peers(self):
+        near = [(self.has(dr, dc), self.at(dr, dc)) for dr, dc in ((-1, 0), (1, 0), (0, -1), (0, 1))]
+        seam = [
+            (self.has(dr, dc) & self.far(dc), self.at(dr, dc)) for dr in (-1, 1) for dc in (-1, 1)
+        ]
+        return near + seam
+
+
+def remote(src, dst, sems, k, device):
+    return pltpu.make_async_remote_copy(
+        src_ref=src,
+        dst_ref=dst,
+        send_sem=sems[0].at[k],
+        recv_sem=sems[1].at[k],
+        device_id=device,
+        device_id_type=MESH,
+    )
+
+
+class Transfers:
+    def __init__(self, entries):
+        self.entries = entries
+
+    def start(self):
+        for sent, received, build in self.entries:
+
+            @pl.when(sent)
+            def _():
+                build().start()
+
+    def wait_recv(self):
+        for sent, received, build in self.entries:
+
+            @pl.when(received)
+            def _():
+                build().wait_recv()
+
+    def wait_send(self):
+        for sent, received, build in self.entries:
+
+            @pl.when(sent)
+            def _():
+                build().wait_send()
+
+
+SIDES = (-1, 1)
 
 
 def clear_edges(row, col, frame):
@@ -115,112 +150,203 @@
         frame[:, 3] = jnp.zeros((2, E, H), jnp.float32)
 
 
-def halo_kernel(re_ref, im_ref, frame, send_sem, recv_sem):
-    row, col = lax.axis_index("sy"), lax.axis_index("sx")
-    greet_neighbours(row, col)
-
-    def make(k, dr, dc, device):
-        rows, count = TILE_ROWS[dr]
-        plane, planes = TILE_PLANES[dc]
-        return [
-            pltpu.make_async_remote_copy(
-                src_ref=source.at[pl.ds(rows - H, count), pl.ds((plane - 1 + n) * H, H)],
-                dst_ref=frame.at[channel, FRAME_PLANES[dc][0] + n, part(FRAME_ROWS[dr])],
-                send_sem=send_sem.at[channel, n, k],
-                recv_sem=recv_sem.at[channel, n, k],
-                device_id=device,
-                device_id_type=MESH,
-            )
-            for channel, source in enumerate((re_ref, im_ref))
-            for n in range(planes)
-        ]
-
-    exchange(row, col, make)
-    clear_edges(row, col, frame)
+def halo(spot, frame, upright, level, corner, seam):
+    def strip(dr, planes, rows_from, to_rows, to_planes, sems, k, device):
+        return lambda: remote(
+            frame.at[:, part(planes), part(rows_from)], frame.at[:, part(to_planes), part(to_rows)], sems, k, device
+        )
+
+    vertical = Transfers(
+        [
+            (
+                spot.has(dr, 0),
+                spot.has(-dr, 0),
+                strip(dr, (1, 2), TILE_ROWS[dr], FRAME_ROWS[dr], (1, 2), upright, k, spot.at(dr, 0)),
+            )
+            for k, dr in enumerate(SIDES)
+        ]
+    )
+    across = Transfers(
+        [
+            (
+                spot.has(dr, dc) & spot.far(dc),
+                spot.has(-dr, -dc) & spot.far(-dc),
+                strip(dr, TILE_PLANES[dc], TILE_ROWS[dr], FRAME_ROWS[dr], FRAME_PLANES[dc], seam, 2 * k + n, spot.at(dr, dc)),
+            )
+            for k, dr in enumerate(SIDES)
+            for n, dc in enumerate(SIDES)
+        ]
+    )
+    middle = Transfers(
+        [
+            (
+                spot.has(0, dc),
+                spot.has(0, -dc),
+                strip(0, TILE_PLANES[dc], (H, F), (H, F), FRAME_PLANES[dc], level, n, spot.at(0, dc)),
+            )
+            for n, dc in enumerate(SIDES)
+        ]
+    )
+    corners = Transfers(
+        [
+            (
+                spot.has(side, 0) & spot.has(0, dc) & ~spot.far(dc),
+                spot.has(side, 0) & spot.has(0, -dc) & ~spot.far(-dc),
+                strip(0, TILE_PLANES[dc], OUTER_ROWS[side], OUTER_ROWS[side], FRAME_PLANES[dc], corner, 2 * k + n, spot.at(0, dc)),
+            )
+            for k, side in enumerate(SIDES)
+            for n, dc in enumerate(SIDES)
+        ]
+    )
+    vertical.start()
+    across.start()
+    middle.start()
+    clear_edges(spot.row, spot.col, frame)
+    vertical.wait_recv()
+    corners.start()
+    for transfers in (middle, across, corners):
+        transfers.wait_recv()
+    for transfers in (vertical, middle, across, corners):
+        transfers.wait_send()
+
+
+def halo_kernel(re_ref, im_ref, frame, *sems):
+    spot = Spot()
     for channel, source in enumerate((re_ref, im_ref)):
         for n in range(2):
             frame[channel, 1 + n, H : H + F] = source[:, n * H : (n + 1) * H]
-    finish(row, col, make)
-
-
-def fold_into(row, col, accum, bufs, send_sem, recv_sem, begin, add):
-    def make(k, dr, dc, device):
-        return [
-            pltpu.make_async_remote_copy(
-                src_ref=accum.at[:, part(OUTER_PLANES[dc]), part(OUTER_ROWS[dr])],
-                dst_ref=bufs[k],
-                send_sem=send_sem.at[k],
-                recv_sem=recv_sem.at[k],
-                device_id=device,
-                device_id_type=MESH,
-            )
-        ]
-
-    exchange(row, col, make)
+    greet(spot.peers())
+    halo(spot, frame, *pairs(sems))
+
+
+def pairs(sems):
+    return [(sems[i], sems[i + 1]) for i in range(0, len(sems), 2)]
+
+
+def fold_parts(spot, accum, cbuf, mbuf, vbuf, fbuf, stack, upright, level, corner, seam):
+    def strip(planes, rows, buf, sems, k, device):
+        return lambda: remote(accum.at[:, part(planes), part(rows)], buf, sems, k, device)
+
+    corners = Transfers(
+        [
+            (
+                spot.has(side, 0) & spot.has(0, dc) & ~spot.far(dc),
+                spot.has(side, 0) & spot.has(0, -dc) & ~spot.far(-dc),
+                strip(OUTER_PLANES[dc], OUTER_ROWS[side], cbuf.at[2 * k + n], corner, 2 * k + n, spot.at(0, dc)),
+            )
+            for k, side in enumerate(SIDES)
+            for n, dc in enumerate(SIDES)
+        ]
+    )
+    across = Transfers(
+        [
+            (
+                spot.has(dr, dc) & spot.far(dc),
+                spot.has(-dr, -dc) & spot.far(-dc),
+                strip(OUTER_PLANES[dc], OUTER_ROWS[dr], fbuf.at[2 * k + n], seam, 2 * k + n, spot.at(dr, dc)),
+            )
+            for k, dr in enumerate(SIDES)
+            for n, dc in enumerate(SIDES)
+        ]
+    )
+    middle = Transfers(
+        [
+            (
+                spot.has(0, dc),
+                spot.has(0, -dc),
+                strip(OUTER_PLANES[dc], (H, F), mbuf.at[n], level, n, spot.at(0, dc)),
+            )
+            for n, dc in enumerate(SIDES)
+        ]
+    )
+    vertical = Transfers(
+        [
+            (
+                spot.has(dr, 0),
+                spot.has(-dr, 0),
+                lambda k=k, dr=dr: remote(stack.at[k], vbuf.at[k], upright, k, spot.at(dr, 0)),
+            )
+            for k, dr in enumerate(SIDES)
+        ]
+    )
+
+    def begin():
+        corners.start()
+        across.start()
+        middle.start()
+
+    def turn():
+        for k, side in enumerate(SIDES):
+            stack[k] = accum[:, 1:3, part(OUTER_ROWS[side])]
+        corners.wait_recv()
+        for (_, received, _), (k, n) in zip(corners.entries, [(k, n) for k in range(2) for n in range(2)]):
+
+            @pl.when(received)
+            def _():
+                plane = INNER_PLANES[SIDES[n]][0] - 1
+                stack[k, :, plane] = stack[k, :, plane] + cbuf[2 * k + n][:, 0]
+
+        vertical.start()
+
+    def end(add):
+        middle.wait_recv()
+        for n, dc in enumerate(SIDES):
+
+            @pl.when(spot.has(0, -dc))
+            def _():
+                add(mbuf.at[n], (H, F), INNER_PLANES[dc])
+
+        vertical.wait_recv()
+        for k, dr in enumerate(SIDES):
+
+            @pl.when(spot.has(-dr, 0))
+            def _():
+                add(vbuf.at[k], INNER_ROWS[dr], (1, 2))
+
+        across.wait_recv()
+        for (_, received, _), (k, n) in zip(across.entries, [(k, n) for k in range(2) for n in range(2)]):
+
+            @pl.when(received)
+            def _():
+                add(fbuf.at[2 * k + n], INNER_ROWS[SIDES[k]], INNER_PLANES[SIDES[n]])
+
+        for transfers in (corners, across, middle, vertical):
+            transfers.wait_send()
+
+    return begin, turn, end
+
+
+def mid_kernel(accum, old, frame, cbuf, mbuf, vbuf, fbuf, stack, *sems):
+    spot = Spot()
+    greet(spot.peers())
+    sems = pairs(sems)
+    begin, turn, end = fold_parts(spot, accum, cbuf, mbuf, vbuf, fbuf, stack, *sems[:4])
     begin()
-    finish(row, col, make)
-    for k, (dr, dc) in enumerate(DIRECTIONS):
-
-        @pl.when(inside(row - dr, col - dc))
-        def _():
-            add(k, INNER_ROWS[dr], INNER_PLANES[dc])
-
-
-def mid_kernel(accum, old, frame, b0, b1, b2, b3, b4, b5, b6, b7, send_sem, recv_sem, send2, recv2):
-    row, col = lax.axis_index("sy"), lax.axis_index("sx")
-    greet_neighbours(row, col)
-    bufs = (b0, b1, b2, b3, b4, b5, b6, b7)
-
-    def begin():
-        clear_edges(row, col, frame)
-        frame[:, 1:3, H : H + F] = old[:, 1:3, H : H + F] + accum[:, 1:3, H : H + F]
-
-    def add(k, rows, planes):
+    frame[:, 1:3, H : H + F] = old[:, 1:3, H : H + F] + accum[:, 1:3, H : H + F]
+    turn()
+
+    def add(buf, rows, planes):
         where = (slice(None), part(planes), part(rows))
-        frame[where] = frame[where] + bufs[k][...]
-
-    fold_into(row, col, accum, bufs, send_sem, recv_sem, begin, add)
-
-    def make(k, dr, dc, device):
-        return [
-            pltpu.make_async_remote_copy(
-                src_ref=frame.at[:, part(TILE_PLANES[dc]), part(TILE_ROWS[dr])],
-                dst_ref=frame.at[:, part(FRAME_PLANES[dc]), part(FRAME_ROWS[dr])],
-                send_sem=send2.at[k],
-                recv_sem=recv2.at[k],
-                device_id=device,
-                device_id_type=MESH,
-            )
-        ]
-
-    exchange(row, col, make)
-    finish(row, col, make)
-
-
-def fold_kernel(accum, old, out_re, out_im, b0, b1, b2, b3, b4, b5, b6, b7, send_sem, recv_sem):
-    row, col = lax.axis_index("sy"), lax.axis_index("sx")
-    greet_neighbours(row, col)
-    bufs = (b0, b1, b2, b3, b4, b5, b6, b7)
-    outs = (out_re, out_im)
-
-    def begin():
-        for channel, out in enumerate(outs):
-            for n in range(2):
-                out[:, n * H : (n + 1) * H] = old[channel, 1 + n, H : H + F] + accum[channel, 1 + n, H : H + F]
-
-    def add(k, rows, planes):
-        for channel, out in enumerate(outs):
-            for n in range(planes[1]):
-                where = (pl.ds(rows[0] - H, rows[1]), pl.ds((planes[0] - 1 + n) * H, H))
-                out[where] = out[where] + bufs[k][channel, n]
-
-    fold_into(row, col, accum, bufs, send_sem, recv_sem, begin, add)
-
-
-def strip_buffers():
+        frame[where] = frame[where] + buf[...]
+
+    end(add)
+    halo(spot, frame, *sems[4:])
+
+
+def fold_buffers():
+    f32 = jnp.float32
     return [
-        pltpu.VMEM((2, OUTER_PLANES[dc][1], OUTER_ROWS[dr][1], H), jnp.float32) for dr, dc in DIRECTIONS
+        pltpu.VMEM((4, 2, 1, H, H), f32),
+        pltpu.VMEM((2, 2, 1, F, H), f32),
+        pltpu.VMEM((2, 2, 2, H, H), f32),
+        pltpu.VMEM((4, 2, 1, H, H), f32),
+        pltpu.VMEM((2, 2, 2, H, H), f32),
     ]
+
+
+def exchange_sems():
+    dma = pltpu.SemaphoreType.DMA
+    return [dma((2,)), dma((2,)), dma((2,)), dma((2,)), dma((4,)), dma((4,)), dma((4,)), dma((4,))]
 
 
 CHUNK1 = 64
@@ -228,7 +354,10 @@
 COLORS = (("x", "y"), ("y", "x"))
 
 
-def sum_kernel(g, probe, out, r0, w0, r1, w1, r2, w2, r3, w4, s0, q0, s1, q1, s2, q2, s3, q3, s4, q4, s5, q5, s6, q6):
+def last_kernel(accum, old, g, probe, out_re, out_im, out, cbuf, mbuf, vbuf, fbuf, stack, *rest):
+    exchange, rest = rest[:8], rest[8:]
+    r0, w0, r1, w1, r2, w2, r3, w4, s0, q0, s1, q1, s2, q2, s3, q3, s4, q4, s5, q5, s6, q6 = rest
+    spot = Spot()
     sy, sx = lax.axis_index("sy"), lax.axis_index("sx")
     here = {
         "y": lax.div(sy, 4),
@@ -255,17 +384,20 @@
         copy.start()
         return copy
 
-    barrier = pltpu.get_barrier_semaphore()
-    for axis in ("core", "x", "y", "z"):
-        for step in range(1, size[axis]):
-            pl.semaphore_signal(barrier, inc=1, device_id=place(axis, step)[1], device_id_type=MESH)
-    pl.semaphore_wait(barrier, 1 + 3 + 3 + 7)
+    begin, turn, end = fold_parts(spot, accum, cbuf, mbuf, vbuf, fbuf, stack, *pairs(exchange))
+    yes = sy >= 0
+    greet(
+        spot.peers()
+        + [(yes, place(axis, step)[1]) for axis in ("core", "x", "y", "z") for step in range(1, size[axis])]
+    )
 
     core = here["core"]
     other, partner = place("core", 1)
     mine = pl.ds(pl.multiple_of(core * 512, 512), 512)
     theirs = pl.ds(pl.multiple_of(other * 512, 512), 512)
-    send(g.at[theirs], r0, s0, q0, partner).wait()
+    first_copy = send(g.at[theirs], r0, s0, q0, partner)
+    begin()
+    first_copy.wait()
     w0[...] = g[mine] + r0[...]
 
     copies = []
@@ -274,6 +406,7 @@
             index, device = place(first, step)
             source = w0.at[pl.ds(pl.multiple_of(c * 256 + index * CHUNK1, CHUNK1), CHUNK1)]
             copies.append(send(source, r1.at[c, step - 1], s1.at[c, step - 1], q1.at[c, step - 1], device))
+    turn()
     for copy in copies:
         copy.wait()
     for c, (first, second) in enumerate(COLORS):
@@ -299,6 +432,18 @@
             copies.append(send(w2.at[c], r3.at[c, here["z"]], s3.at[c, step - 1], q3.at[c, step - 1], device))
     for c in range(2):
         r3[c, here["z"]] = w2[c]
+    outs = (out_re, out_im)
+    for channel, tile in enumerate(outs):
+        for n in range(2):
+            tile[:, n * H : (n + 1) * H] = old[channel, 1 + n, H : H + F] + accum[channel, 1 + n, H : H + F]
+
+    def add(buf, rows, planes):
+        for channel, tile in enumerate(outs):
+            for n in range(planes[1]):
+                where = (pl.ds(rows[0] - H, rows[1]), pl.ds((planes[0] - 1 + n) * H, H))
+                tile[where] = tile[where] + buf[channel, n]
+
+    end(add)
     for copy in copies:
         copy.wait()
     for c, (first, second) in enumerate(COLORS):
@@ -458,20 +603,18 @@
             cost_estimate=pl.CostEstimate(flops=4_300_000_000, bytes_accessed=10_000_000, transcendentals=262144),
         )(*ins)
 
-    frame = comm(halo_kernel, frame_shape, [dma((2, 2, 8)), dma((2, 2, 8))], 0, 2)(object_re, object_im)
+    frame = comm(halo_kernel, frame_shape, exchange_sems(), 0, 2)(object_re, object_im)
     accum, grad = work(0, frame, None)
-    frame = comm(
-        mid_kernel, frame_shape, strip_buffers() + [dma((8,))] * 4, 1, 2
-    )(accum, frame)
+    frame = comm(mid_kernel, frame_shape, fold_buffers() + exchange_sems() + exchange_sems(), 1, 2)(accum, frame)
     accum, grad = work(1, frame, grad)
-    out = comm(
-        fold_kernel, [jax.ShapeDtypeStruct((F, F), f32)] * 2, strip_buffers() + [dma((8,))] * 2, 2, 2
-    )(accum, frame)
     probe = jnp.stack([probe_re, probe_im])
-    flat = comm(
-        sum_kernel,
-        jax.ShapeDtypeStruct((1024, F), f32),
-        [
+    tile_shape = jax.ShapeDtypeStruct((F, F), f32)
+    out_re, out_im, flat = comm(
+        last_kernel,
+        [tile_shape, tile_shape, jax.ShapeDtypeStruct((1024, F), f32)],
+        fold_buffers()
+        + exchange_sems()
+        + [
             pltpu.VMEM((512, F), f32),
             pltpu.VMEM((512, F), f32),
             pltpu.VMEM((2, 3, CHUNK1, F), f32),
@@ -488,11 +631,11 @@
             dma((2, 3)), dma((2, 3)),
             dma, dma,
         ],
-        3,
         2,
-    )(grad.reshape(1024, F), probe.reshape(1024, F))
+        4,
+    )(accum, frame, grad.reshape(1024, F), probe.reshape(1024, F))
     new = flat.reshape(2, 2, F, F)
-    return (out[0], out[1], new[0], new[1])
+    return (out_re, out_im, new[0], new[1])
 
 
 def solution(mesh):

time: 215 us -> 165 us (0.77)
  Pallas kernels: 208 us -> 159 us
    pallas_call x4 -> x3, Pallas kernels: 185 us -> 136 us  [the longest x1 77.4 us: local(): comm(last_kernel, [tile_shape, tile_shape, jax.ShapeDtypeStruct((1024, F)...]
where the time goes in v1:
time: 165 us
  Pallas kernels  159 us (96%)
  local copies, waits for them, and re-layouts  4.39 us (3%)
    pallas_call x1, Pallas kernels, local(): comm(last_kernel, [tile_shape, tile_shape, jax.ShapeDtypeStruct((1024, F)...  77.4 us
    pallas_call x1, Pallas kernels, local(): comm(mid_kernel, frame_shape, fold_buffers() + exchange_sems() + exchange...  40.2 us
    pallas_call x2, Pallas kernels, work(): pl.pallas_call(functools.partial(work_kernel, batch), out_shape=[frame_sh...  23.5 us
    pallas_call x1, Pallas kernels, local(): comm(halo_kernel, frame_shape, exchange_sems(), 0, 2)(object_re, object_im)  18 us

profile of v1, /device:TPU:1, one launch (start us, length us, event | category | flops | bytes accessed | tf_op | source)
XLA Modules:
  0.0 165.3 jit_solution(8058371919156789824)
XLA Ops:
  0.6 0.0 copy-start.4
  0.6 18.0 %shard_map.138.frame.old = f32[2,4,512,128]{3,2,1,0:T(8,128)} custom-call(f32[256,256]{1,0:T(8,128)} %re_ref.1, f32[256,256]{1,0:T(8,128)} %im_ref.1), custom_call_target="tpu_custom_call" | custom-call | tf_op jit(solution)/shard_map/pallas_call | solution.py:606
  18.6 0.0 copy-done.4
  18.6 0.7 copy.16.offsets
  19.3 11.6 %shard_map.139 = (f32[2,4,512,128]{3,2,1,0:T(8,128)}, f32[2,2,256,256]{3,2,1,0:T(8,128)}) custom-call(s32[8]{0:T(128)} %bitcast.18, s32[8,2]{1,0:T(8,128)} %copy.16.offsets, f32[2,4,512,128]{3,2,1,0:T(8,128)} %shard_map.138.frame.old, f32[2,256,256]{2,1,0:T(8,128)} %probe_re.3, f32[2,256,256]{2,1,0:T(8,128)} %probe_im.3, f32[8,256,256]{2,1,0:T(8,128)} %bitcast.16, ...), custom_call_target="tpu_custom_call" | custom-call | flops 4300000256 | bytes 10000000 | tf_op jit(solution)/shard_map/pallas_call | solution.py:590
  30.9 40.2 %shard_map.140.frame.old = f32[2,4,512,128]{3,2,1,0:T(8,128)} custom-call(f32[2,4,512,128]{3,2,1,0:T(8,128)} %get-tuple-element.11.accum, f32[2,4,512,128]{3,2,1,0:T(8,128)} %shard_map.138.frame.old), custom_call_target="tpu_custom_call" | custom-call | tf_op jit(solution)/shard_map/pallas_call | solution.py:608
  71.2 0.0 copy-start
  71.2 0.0 copy-start.1
  71.2 11.9 %shard_map.141 = (f32[2,4,512,128]{3,2,1,0:T(8,128)}, f32[2,2,256,256]{3,2,1,0:T(8,128)}) custom-call(s32[8]{0:T(128)} %bitcast.19, s32[8,2]{1,0:T(8,128)} %copy.16.offsets, f32[2,4,512,128]{3,2,1,0:T(8,128)} %shard_map.140.frame.old, f32[2,256,256]{2,1,0:T(8,128)} %probe_re.3, f32[2,256,256]{2,1,0:T(8,128)} %probe_im.3, f32[8,256,256]{2,1,0:T(8,128)} %bitcast.17, ...), custom_call_target="tpu_custom_call" | custom-call | flops 4300000256 | bytes 10000000 | tf_op jit(solution)/shard_map/pallas_call | solution.py:590
  83.1 0.0 copy-done
  83.1 0.0 copy-done.1
  83.1 1.1 pad_maximum_fusion
  84.2 77.4 %shard_map.142 = (f32[256,256]{1,0:T(8,128)}, f32[256,256]{1,0:T(8,128)}, f32[1024,256]{1,0:T(8,128)}) custom-call(f32[2,4,512,128]{3,2,1,0:T(8,128)} %get-tuple-element.13.accum, f32[2,4,512,128]{3,2,1,0:T(8,128)} %shard_map.140.frame.old, f32[1024,256]{1,0:T(8,128)} %bitcast.10, f32[1024,256]{1,0:T(8,128)} %bitcast.9), custom_call_target="tpu_custom_call" | custom-call | tf_op jit(solution)/shard_map/pallas_call | solution.py:612
  161.6 0.0 copy-start.3
  161.6 0.0 copy-start.2
  161.6 2.3 %fusion = (f32[512,256]{1,0:T(8,128)}, f32[512,256]{1,0:T(8,128)}) fusion(f32[1024,256]{1,0:T(8,128)} %get-tuple-element.17), kind=kLoop, calls=%fused_computation.1 | loop fusion | bytes 2097152 | tf_op jit(solution)/shard_map/slice | solution.py:638
  163.9 0.0 copy-done.3
  163.9 0.7 copy.19
  164.6 0.0 copy-done.2
  164.6 0.7 copy.20
Async XLA Ops:
  0.6 18.0 %copy-start.4 = (s32[1,1,8,2]{2,3,1,0:T(2,128)S(1)}, s32[1,1,8,2]{2,3,1,0:T(2,128)}, u32[]{:S(2)}) copy-start(s32[1,1,8,2]{2,3,1,0:T(2,128)} %param.16) | copy-start | bytes 196
  71.2 11.9 %copy-start = (f32[2,256,256]{2,1,0:T(8,128)S(1)}, f32[2,256,256]{2,1,0:T(8,128)}, u32[]{:S(2)}) copy-start(f32[2,256,256]{2,1,0:T(8,128)} %probe_re.3) | copy-start | bytes 1572868
  71.2 11.9 %copy-start.1 = (f32[2,256,256]{2,1,0:T(8,128)S(1)}, f32[2,256,256]{2,1,0:T(8,128)}, u32[]{:S(2)}) copy-start(f32[2,256,256]{2,1,0:T(8,128)} %probe_im.3) | copy-start | bytes 1572868
  161.6 2.3 %copy-start.3 = (f32[256,256]{1,0:T(8,128)S(1)}, f32[256,256]{1,0:T(8,128)}, u32[]{:S(2)}) copy-start(f32[256,256]{1,0:T(8,128)} %get-tuple-element.24) | copy-start | bytes 786436
  161.6 3.0 %copy-start.2 = (f32[256,256]{1,0:T(8,128)S(1)}, f32[256,256]{1,0:T(8,128)}, u32[]{:S(2)}) copy-start(f32[256,256]{1,0:T(8,128)} %get-tuple-element.25) | copy-start | bytes 786436

commit v2 on v1

--- a/solution.py
+++ b/solution.py
@@ -74,6 +74,11 @@
 class Spot:
     def __init__(self):
         self.row, self.col = lax.axis_index("sy"), lax.axis_index("sx")
+        self.half = lax.div(self.col, SEAM)
+        self.seat = lax.rem(self.col, SEAM)
+        self.seam = (self.col == SEAM - 1) | (self.col == SEAM)
+        self.edge = (self.row, SEAM - 1 + self.half)
+        self.beyond = (self.row, SEAM - self.half)
 
     def at(self, dr, dc):
         return (self.row + dr, self.col + dc)
@@ -86,18 +91,25 @@
 
     def peers(self):
         near = [(self.has(dr, dc), self.at(dr, dc)) for dr, dc in ((-1, 0), (1, 0), (0, -1), (0, 1))]
-        seam = [
+        diagonal = [
             (self.has(dr, dc) & self.far(dc), self.at(dr, dc)) for dr in (-1, 1) for dc in (-1, 1)
         ]
-        return near + seam
-
-
-def remote(src, dst, sems, k, device):
+        row, col = self.row, self.col
+        relays = [
+            (self.seam & (col != c) & (jnp.abs(col - c) != 1), (row, jnp.int32(c))) for c in range(COLS)
+        ]
+        edges = [(~self.seam & (jnp.abs(col - c) != 1), (row, jnp.int32(c))) for c in (SEAM - 1, SEAM)]
+        return near + diagonal + relays[: SEAM - 1] + relays[SEAM + 1 :] + [
+            (self.seam & (there), device) for there, device in relays[SEAM - 1 : SEAM + 1]
+        ] + edges
+
+
+def remote(src, dst, sems, at, device):
     return pltpu.make_async_remote_copy(
         src_ref=src,
         dst_ref=dst,
-        send_sem=sems[0].at[k],
-        recv_sem=sems[1].at[k],
+        send_sem=sems[0].at[at],
+        recv_sem=sems[1].at[at],
         device_id=device,
         device_id_type=MESH,
     )
@@ -150,203 +162,329 @@
         frame[:, 3] = jnp.zeros((2, E, H), jnp.float32)
 
 
-def halo(spot, frame, upright, level, corner, seam):
-    def strip(dr, planes, rows_from, to_rows, to_planes, sems, k, device):
-        return lambda: remote(
-            frame.at[:, part(planes), part(rows_from)], frame.at[:, part(to_planes), part(to_rows)], sems, k, device
+FOUR = [(k, n) for k in range(2) for n in range(2)]
+SLICE = F // SEAM
+
+
+class Relay:
+    def __init__(self, spot, source, target, held, first, second):
+        self.spot, self.source, self.target, self.held = spot, source, target, held
+        self.first, self.second = first, second
+
+    def out(self, q):
+        spot = self.spot
+        device = (spot.row, spot.half * SEAM + q)
+        return remote(self.source(q * SLICE), self.held, self.first, q, device)
+
+    def arrive(self):
+        return pltpu.make_async_remote_copy(
+            src_ref=self.held, dst_ref=self.held, send_sem=self.first[0].at[0],
+            recv_sem=self.first[1].at[self.spot.seat], device_id=self.spot.edge, device_id_type=MESH,
         )
 
-    vertical = Transfers(
-        [
+    def on(self, q, src):
+        return remote(src, self.target(pl.multiple_of(q * SLICE, SLICE)), self.second, q, self.spot.beyond)
+
+    def start(self):
+        spot = self.spot
+        for q in range(SEAM):
+
+            @pl.when(spot.seam & (spot.seat != q))
+            def _():
+                self.out(q).start()
+
+        for half, q in ((0, SEAM - 1), (1, 0)):
+
+            @pl.when(spot.seam & (spot.half == half))
+            def _():
+                self.on(q, self.source(q * SLICE)).start()
+
+    def turn(self):
+        @pl.when(~self.spot.seam)
+        def _():
+            self.arrive().wait_recv()
+            self.on(self.spot.seat, self.held).start()
+
+    def wait_recv(self):
+        @pl.when(self.spot.seam)
+        def _():
+            for q in range(SEAM):
+                self.on(q, self.held).wait_recv()
+
+    def wait_send(self):
+        spot = self.spot
+
+        @pl.when(~spot.seam)
+        def _():
+            self.on(spot.seat, self.held).wait_send()
+
+        for q in range(SEAM):
+
+            @pl.when(spot.seam & (spot.seat != q))
+            def _():
+                self.out(q).wait_send()
+
+        for half, q in ((0, SEAM - 1), (1, 0)):
+
+            @pl.when(spot.seam & (spot.half == half))
+            def _():
+                self.on(q, self.held).wait_send()
+
+
+class Halo:
+    def __init__(self, spot, frame, held, upright, level, corner, seam, first, second):
+        self.spot, self.frame = spot, frame
+
+        def strip(ch, dr, planes, rows_from, to_rows, to_planes, sems, k, device):
+            c = pl.ds(ch, 1)
+            return lambda: remote(
+                frame.at[c, part(planes), part(rows_from)], frame.at[c, part(to_planes), part(to_rows)], sems, (ch, k), device
+            )
+
+        def both(make):
+            return [Transfers(make(ch)) for ch in range(2)]
+
+        self.vertical = both(lambda ch: [
             (
                 spot.has(dr, 0),
                 spot.has(-dr, 0),
-                strip(dr, (1, 2), TILE_ROWS[dr], FRAME_ROWS[dr], (1, 2), upright, k, spot.at(dr, 0)),
+                strip(ch, dr, (1, 2), TILE_ROWS[dr], FRAME_ROWS[dr], (1, 2), upright, k, spot.at(dr, 0)),
             )
             for k, dr in enumerate(SIDES)
-        ]
-    )
-    across = Transfers(
-        [
+        ])
+        self.across = both(lambda ch: [
             (
                 spot.has(dr, dc) & spot.far(dc),
                 spot.has(-dr, -dc) & spot.far(-dc),
-                strip(dr, TILE_PLANES[dc], TILE_ROWS[dr], FRAME_ROWS[dr], FRAME_PLANES[dc], seam, 2 * k + n, spot.at(dr, dc)),
+                strip(ch, dr, TILE_PLANES[dc], TILE_ROWS[dr], FRAME_ROWS[dr], FRAME_PLANES[dc], seam, 2 * k + n, spot.at(dr, dc)),
             )
             for k, dr in enumerate(SIDES)
             for n, dc in enumerate(SIDES)
-        ]
-    )
-    middle = Transfers(
-        [
+        ])
+        self.middle = both(lambda ch: [
             (
-                spot.has(0, dc),
-                spot.has(0, -dc),
-                strip(0, TILE_PLANES[dc], (H, F), (H, F), FRAME_PLANES[dc], level, n, spot.at(0, dc)),
+                spot.has(0, dc) & ~spot.far(dc),
+                spot.has(0, -dc) & ~spot.far(-dc),
+                strip(ch, 0, TILE_PLANES[dc], (H, F), (H, F), FRAME_PLANES[dc], level, n, spot.at(0, dc)),
             )
             for n, dc in enumerate(SIDES)
-        ]
-    )
-    corners = Transfers(
-        [
+        ])
+        self.corners = both(lambda ch: [
             (
                 spot.has(side, 0) & spot.has(0, dc) & ~spot.far(dc),
                 spot.has(side, 0) & spot.has(0, -dc) & ~spot.far(-dc),
-                strip(0, TILE_PLANES[dc], OUTER_ROWS[side], OUTER_ROWS[side], FRAME_PLANES[dc], corner, 2 * k + n, spot.at(0, dc)),
+                strip(ch, 0, TILE_PLANES[dc], OUTER_ROWS[side], OUTER_ROWS[side], FRAME_PLANES[dc], corner, 2 * k + n, spot.at(0, dc)),
             )
             for k, side in enumerate(SIDES)
             for n, dc in enumerate(SIDES)
-        ]
-    )
-    vertical.start()
-    across.start()
-    middle.start()
-    clear_edges(spot.row, spot.col, frame)
-    vertical.wait_recv()
-    corners.start()
-    for transfers in (middle, across, corners):
-        transfers.wait_recv()
-    for transfers in (vertical, middle, across, corners):
-        transfers.wait_send()
-
-
-def halo_kernel(re_ref, im_ref, frame, *sems):
+        ])
+        half = spot.half
+        self.relay = Relay(
+            spot,
+            lambda row: frame.at[:, pl.ds(2 - half, 1), pl.ds(H + row, SLICE)],
+            lambda row: frame.at[:, pl.ds(3 * half, 1), pl.ds(H + row, SLICE)],
+            held, first, second,
+        )
+
+    def begin(self, ch):
+        self.vertical[ch].start()
+        self.across[ch].start()
+
+    def aside(self):
+        self.relay.start()
+        self.middle[0].start()
+        self.middle[1].start()
+        self.relay.turn()
+
+    def end(self):
+        for ch in range(2):
+            self.vertical[ch].wait_recv()
+            self.corners[ch].start()
+        for ch in range(2):
+            self.middle[ch].wait_recv()
+        self.relay.wait_recv()
+        for ch in range(2):
+            for transfers in (self.across[ch], self.corners[ch]):
+                transfers.wait_recv()
+        for ch in range(2):
+            for transfers in (self.vertical[ch], self.middle[ch], self.across[ch], self.corners[ch]):
+                transfers.wait_send()
+        self.relay.wait_send()
+
+
+def halo_kernel(re_ref, im_ref, frame, held, *sems):
     spot = Spot()
     for channel, source in enumerate((re_ref, im_ref)):
         for n in range(2):
             frame[channel, 1 + n, H : H + F] = source[:, n * H : (n + 1) * H]
     greet(spot.peers())
-    halo(spot, frame, *pairs(sems))
+    halo = Halo(spot, frame, held, *pairs(sems))
+    halo.begin(0)
+    halo.begin(1)
+    halo.aside()
+    clear_edges(spot.row, spot.col, frame)
+    halo.end()
 
 
 def pairs(sems):
     return [(sems[i], sems[i + 1]) for i in range(0, len(sems), 2)]
 
 
-def fold_parts(spot, accum, cbuf, mbuf, vbuf, fbuf, stack, upright, level, corner, seam):
-    def strip(planes, rows, buf, sems, k, device):
-        return lambda: remote(accum.at[:, part(planes), part(rows)], buf, sems, k, device)
-
-    corners = Transfers(
-        [
+class Fold:
+    def __init__(self, spot, accum, cbuf, mbuf, vbuf, fbuf, stack, held, upright, level, corner, seam, first, second):
+        self.spot, self.accum, self.stack = spot, accum, stack
+        self.cbuf, self.mbuf, self.vbuf, self.fbuf = cbuf, mbuf, vbuf, fbuf
+
+        def strip(ch, planes, rows, buf, sems, k, device):
+            return lambda: remote(accum.at[ch, part(planes), part(rows)], buf.at[ch, k], sems, (ch, k), device)
+
+        def both(make):
+            return [Transfers(make(ch)) for ch in range(2)]
+
+        self.corners = both(lambda ch: [
             (
                 spot.has(side, 0) & spot.has(0, dc) & ~spot.far(dc),
                 spot.has(side, 0) & spot.has(0, -dc) & ~spot.far(-dc),
-                strip(OUTER_PLANES[dc], OUTER_ROWS[side], cbuf.at[2 * k + n], corner, 2 * k + n, spot.at(0, dc)),
+                strip(ch, OUTER_PLANES[dc], OUTER_ROWS[side], cbuf, corner, 2 * k + n, spot.at(0, dc)),
             )
             for k, side in enumerate(SIDES)
             for n, dc in enumerate(SIDES)
-        ]
-    )
-    across = Transfers(
-        [
+        ])
+        self.across = both(lambda ch: [
             (
                 spot.has(dr, dc) & spot.far(dc),
                 spot.has(-dr, -dc) & spot.far(-dc),
-                strip(OUTER_PLANES[dc], OUTER_ROWS[dr], fbuf.at[2 * k + n], seam, 2 * k + n, spot.at(dr, dc)),
+                strip(ch, OUTER_PLANES[dc], OUTER_ROWS[dr], fbuf, seam, 2 * k + n, spot.at(dr, dc)),
             )
             for k, dr in enumerate(SIDES)
             for n, dc in enumerate(SIDES)
-        ]
-    )
-    middle = Transfers(
-        [
+        ])
+        self.middle = both(lambda ch: [
             (
-                spot.has(0, dc),
-                spot.has(0, -dc),
-                strip(OUTER_PLANES[dc], (H, F), mbuf.at[n], level, n, spot.at(0, dc)),
+                spot.has(0, dc) & ~spot.far(dc),
+                spot.has(0, -dc) & ~spot.far(-dc),
+                strip(ch, OUTER_PLANES[dc], (H, F), mbuf, level, n, spot.at(0, dc)),
             )
             for n, dc in enumerate(SIDES)
-        ]
-    )
-    vertical = Transfers(
-        [
+        ])
+        self.vertical = both(lambda ch: [
             (
                 spot.has(dr, 0),
                 spot.has(-dr, 0),
-                lambda k=k, dr=dr: remote(stack.at[k], vbuf.at[k], upright, k, spot.at(dr, 0)),
+                lambda k=k, dr=dr: remote(stack.at[ch, k], vbuf.at[ch, k], upright, (ch, k), spot.at(dr, 0)),
             )
             for k, dr in enumerate(SIDES)
-        ]
-    )
-
-    def begin():
-        corners.start()
-        across.start()
-        middle.start()
-
-    def turn():
+        ])
+        half = spot.half
+        self.relay = Relay(
+            spot,
+            lambda row: accum.at[:, pl.ds(3 - 3 * half, 1), pl.ds(H + row, SLICE)],
+            lambda row: mbuf.at[:, 1 - half, :, pl.ds(row, SLICE)],
+            held, first, second,
+        )
+
+    def begin(self):
+        self.corners[0].start()
+        self.corners[1].start()
+
+    def aside(self):
+        self.relay.start()
+        self.middle[0].start()
+        self.middle[1].start()
+
+    def turn(self, ch):
+        stack, cbuf = self.stack, self.cbuf
         for k, side in enumerate(SIDES):
-            stack[k] = accum[:, 1:3, part(OUTER_ROWS[side])]
-        corners.wait_recv()
-        for (_, received, _), (k, n) in zip(corners.entries, [(k, n) for k in range(2) for n in range(2)]):
+            stack[ch, k] = self.accum[ch, 1:3, part(OUTER_ROWS[side])]
+        self.corners[ch].wait_recv()
+        for (_, received, _), (k, n) in zip(self.corners[ch].entries, FOUR):
 
             @pl.when(received)
             def _():
                 plane = INNER_PLANES[SIDES[n]][0] - 1
-                stack[k, :, plane] = stack[k, :, plane] + cbuf[2 * k + n][:, 0]
-
-        vertical.start()
-
-    def end(add):
-        middle.wait_recv()
+                stack[ch, k, plane] = stack[ch, k, plane] + cbuf[ch, 2 * k + n, 0]
+
+        self.vertical[ch].start()
+        self.across[ch].start()
+
+    def end(self, ch, add):
+        spot = self.spot
+        self.middle[ch].wait_recv()
+        if ch == 0:
+            self.relay.wait_recv()
         for n, dc in enumerate(SIDES):
 
             @pl.when(spot.has(0, -dc))
             def _():
-                add(mbuf.at[n], (H, F), INNER_PLANES[dc])
-
-        vertical.wait_recv()
+                add(self.mbuf.at[ch, n], (H, F), INNER_PLANES[dc])
+
+        self.vertical[ch].wait_recv()
         for k, dr in enumerate(SIDES):
 
             @pl.when(spot.has(-dr, 0))
             def _():
-                add(vbuf.at[k], INNER_ROWS[dr], (1, 2))
-
-        across.wait_recv()
-        for (_, received, _), (k, n) in zip(across.entries, [(k, n) for k in range(2) for n in range(2)]):
+                add(self.vbuf.at[ch, k], INNER_ROWS[dr], (1, 2))
+
+        self.across[ch].wait_recv()
+        for (_, received, _), (k, n) in zip(self.across[ch].entries, FOUR):
 
             @pl.when(received)
             def _():
-                add(fbuf.at[2 * k + n], INNER_ROWS[SIDES[k]], INNER_PLANES[SIDES[n]])
-
-        for transfers in (corners, across, middle, vertical):
-            transfers.wait_send()
-
-    return begin, turn, end
-
-
-def mid_kernel(accum, old, frame, cbuf, mbuf, vbuf, fbuf, stack, *sems):
+                add(self.fbuf.at[ch, 2 * k + n], INNER_ROWS[SIDES[k]], INNER_PLANES[SIDES[n]])
+
+    def close(self):
+        for ch in range(2):
+            for transfers in (self.corners[ch], self.across[ch], self.middle[ch], self.vertical[ch]):
+                transfers.wait_send()
+        self.relay.wait_send()
+
+
+def mid_kernel(accum, old, frame, cbuf, mbuf, vbuf, fbuf, stack, held, held2, *sems):
     spot = Spot()
     greet(spot.peers())
     sems = pairs(sems)
-    begin, turn, end = fold_parts(spot, accum, cbuf, mbuf, vbuf, fbuf, stack, *sems[:4])
-    begin()
+    fold = Fold(spot, accum, cbuf, mbuf, vbuf, fbuf, stack, held, *sems[:6])
+    halo = Halo(spot, frame, held2, *sems[6:])
+    fold.begin()
+    fold.aside()
+    fold.turn(0)
+    fold.turn(1)
+    fold.relay.turn()
+    clear_edges(spot.row, spot.col, frame)
     frame[:, 1:3, H : H + F] = old[:, 1:3, H : H + F] + accum[:, 1:3, H : H + F]
-    turn()
-
-    def add(buf, rows, planes):
-        where = (slice(None), part(planes), part(rows))
-        frame[where] = frame[where] + buf[...]
-
-    end(add)
-    halo(spot, frame, *sems[4:])
+    for ch in range(2):
+
+        def add(buf, rows, planes):
+            where = (ch, part(planes), part(rows))
+            frame[where] = frame[where] + buf[...]
+
+        fold.end(ch, add)
+        halo.begin(ch)
+    halo.aside()
+    halo.end()
+    fold.close()
+
+
+def held_buffer():
+    return pltpu.VMEM((2, 1, SLICE, H), jnp.float32)
 
 
 def fold_buffers():
     f32 = jnp.float32
     return [
-        pltpu.VMEM((4, 2, 1, H, H), f32),
+        pltpu.VMEM((2, 4, 1, H, H), f32),
         pltpu.VMEM((2, 2, 1, F, H), f32),
         pltpu.VMEM((2, 2, 2, H, H), f32),
-        pltpu.VMEM((4, 2, 1, H, H), f32),
+        pltpu.VMEM((2, 4, 1, H, H), f32),
         pltpu.VMEM((2, 2, 2, H, H), f32),
+        held_buffer(),
     ]
 
 
 def exchange_sems():
     dma = pltpu.SemaphoreType.DMA
-    return [dma((2,)), dma((2,)), dma((2,)), dma((2,)), dma((4,)), dma((4,)), dma((4,)), dma((4,))]
+    shapes = ((2, 2), (2, 2), (2, 4), (2, 4), (SEAM,), (SEAM,))
+    return [dma(shape) for shape in shapes for _ in range(2)]
 
 
 CHUNK1 = 64
@@ -354,8 +492,8 @@
 COLORS = (("x", "y"), ("y", "x"))
 
 
-def last_kernel(accum, old, g, probe, out_re, out_im, out, cbuf, mbuf, vbuf, fbuf, stack, *rest):
-    exchange, rest = rest[:8], rest[8:]
+def last_kernel(accum, old, g, probe_re, probe_im, out_re, out_im, out, cbuf, mbuf, vbuf, fbuf, stack, held, *rest):
+    exchange, rest = rest[:12], rest[12:]
     r0, w0, r1, w1, r2, w2, r3, w4, s0, q0, s1, q1, s2, q2, s3, q3, s4, q4, s5, q5, s6, q6 = rest
     spot = Spot()
     sy, sx = lax.axis_index("sy"), lax.axis_index("sx")
@@ -384,7 +522,7 @@
         copy.start()
         return copy
 
-    begin, turn, end = fold_parts(spot, accum, cbuf, mbuf, vbuf, fbuf, stack, *pairs(exchange))
+    fold = Fold(spot, accum, cbuf, mbuf, vbuf, fbuf, stack, held, *pairs(exchange))
     yes = sy >= 0
     greet(
         spot.peers()
@@ -396,7 +534,6 @@
     mine = pl.ds(pl.multiple_of(core * 512, 512), 512)
     theirs = pl.ds(pl.multiple_of(other * 512, 512), 512)
     first_copy = send(g.at[theirs], r0, s0, q0, partner)
-    begin()
     first_copy.wait()
     w0[...] = g[mine] + r0[...]
 
@@ -406,7 +543,7 @@
             index, device = place(first, step)
             source = w0.at[pl.ds(pl.multiple_of(c * 256 + index * CHUNK1, CHUNK1), CHUNK1)]
             copies.append(send(source, r1.at[c, step - 1], s1.at[c, step - 1], q1.at[c, step - 1], device))
-    turn()
+    fold.begin()
     for copy in copies:
         copy.wait()
     for c, (first, second) in enumerate(COLORS):
@@ -432,24 +569,22 @@
             copies.append(send(w2.at[c], r3.at[c, here["z"]], s3.at[c, step - 1], q3.at[c, step - 1], device))
     for c in range(2):
         r3[c, here["z"]] = w2[c]
+    fold.turn(0)
+    fold.turn(1)
+    fold.aside()
+    fold.relay.turn()
     outs = (out_re, out_im)
     for channel, tile in enumerate(outs):
         for n in range(2):
             tile[:, n * H : (n + 1) * H] = old[channel, 1 + n, H : H + F] + accum[channel, 1 + n, H : H + F]
 
-    def add(buf, rows, planes):
-        for channel, tile in enumerate(outs):
-            for n in range(planes[1]):
-                where = (pl.ds(rows[0] - H, rows[1]), pl.ds((planes[0] - 1 + n) * H, H))
-                tile[where] = tile[where] + buf[channel, n]
-
-    end(add)
     for copy in copies:
         copy.wait()
     for c, (first, second) in enumerate(COLORS):
         total = ((r3[c, 0] + r3[c, 1]) + (r3[c, 2] + r3[c, 3])) + ((r3[c, 4] + r3[c, 5]) + (r3[c, 6] + r3[c, 7]))
-        start = core * 512 + c * 256 + here[first] * CHUNK1 + here[second] * CHUNK2
-        base = probe[pl.ds(pl.multiple_of(start, CHUNK2), CHUNK2)]
+        start = c * 256 + here[first] * CHUNK1 + here[second] * CHUNK2
+        spots = pl.ds(pl.multiple_of(start, CHUNK2), CHUNK2)
+        base = jnp.where(core == 0, probe_re[spots], probe_im[spots])
         w4[c, pl.ds(pl.multiple_of(here[second] * CHUNK2, CHUNK2), CHUNK2)] = base + rate * total
 
     copies = []
@@ -472,7 +607,25 @@
     for copy in copies:
         copy.wait()
 
-    send(out.at[mine], out.at[mine], s6, q6, partner).wait()
+    last_copy = send(out.at[mine], out.at[mine], s6, q6, partner)
+    for ch, tile in enumerate(outs):
+
+        def add(buf, rows, planes):
+            for n in range(planes[1]):
+                where = (pl.ds(rows[0] - H, rows[1]), pl.ds((planes[0] - 1 + n) * H, H))
+                tile[where] = tile[where] + buf[n]
+
+        fold.end(ch, add)
+    fold.close()
+    last_copy.wait()
+
+
+def write_kernel(a, b, flat, out_a, out_b, out_c, out_d):
+    out_a[...] = a[...]
+    out_b[...] = b[...]
+    for m in range(2):
+        out_c[m] = flat[m * F : (m + 1) * F]
+        out_d[m] = flat[(2 + m) * F : (3 + m) * F]
 
 
 def work_kernel(batch, order, offsets, frame, probe_re, probe_im, amps, left, back_left, right, back_right, *rest):
@@ -603,11 +756,10 @@
             cost_estimate=pl.CostEstimate(flops=4_300_000_000, bytes_accessed=10_000_000, transcendentals=262144),
         )(*ins)
 
-    frame = comm(halo_kernel, frame_shape, exchange_sems(), 0, 2)(object_re, object_im)
+    frame = comm(halo_kernel, frame_shape, [held_buffer()] + exchange_sems(), 0, 2)(object_re, object_im)
     accum, grad = work(0, frame, None)
-    frame = comm(mid_kernel, frame_shape, fold_buffers() + exchange_sems() + exchange_sems(), 1, 2)(accum, frame)
+    frame = comm(mid_kernel, frame_shape, fold_buffers() + [held_buffer()] + exchange_sems() + exchange_sems(), 1, 2)(accum, frame)
     accum, grad = work(1, frame, grad)
-    probe = jnp.stack([probe_re, probe_im])
     tile_shape = jax.ShapeDtypeStruct((F, F), f32)
     out_re, out_im, flat = comm(
         last_kernel,
@@ -632,10 +784,17 @@
             dma, dma,
         ],
         2,
-        4,
-    )(accum, frame, grad.reshape(1024, F), probe.reshape(1024, F))
-    new = flat.reshape(2, 2, F, F)
-    return (out_re, out_im, new[0], new[1])
+        5,
+    )(accum, frame, grad.reshape(1024, F), probe_re.reshape(512, F), probe_im.reshape(512, F))
+    probe_shape = jax.ShapeDtypeStruct((2, F, F), f32)
+    return tuple(
+        pl.pallas_call(
+            write_kernel,
+            out_shape=[tile_shape, tile_shape, probe_shape, probe_shape],
+            in_specs=[VMEM] * 3,
+            out_specs=[VMEM] * 4,
+        )(out_re, out_im, flat)
+    )
 
 
 def solution(mesh):

time: 165 us -> 156 us (0.945)
  Pallas kernels: 159 us -> 154 us
  local copies, waits for them, and re-layouts: 4.39 us -> 1.35 us
    pallas_call x1, Pallas kernels: 77.4 us -> 53.2 us  [local(): comm(last_kernel, [tile_shape, tile_shape, jax.ShapeDtypeStruct((1024, F)...]
    pallas_call x2 -> x3, Pallas kernels: 58.2 us -> 77.1 us  [the longest x1 48.8 us: local(): comm(mid_kernel, frame_shape, fold_buffers() + [held_buffer()] + exchange...]
    slice x1 -> x0, local copies, waits for them, and re-layouts: 2.29 us -> none  [local(): return (out_re, out_im, new[0], new[1])]
where the time goes in v2:
time: 156 us
  Pallas kernels  154 us (99%)
    pallas_call x1, Pallas kernels, local(): comm(last_kernel, [tile_shape, tile_shape, jax.ShapeDtypeStruct((1024, F)...  53.2 us
    pallas_call x1, Pallas kernels, local(): comm(mid_kernel, frame_shape, fold_buffers() + [held_buffer()] + exchange...  48.8 us
    pallas_call x1, Pallas kernels, local(): comm(halo_kernel, frame_shape, [held_buffer()] + exchange_sems(), 0, 2)  25.7 us
    pallas_call x2, Pallas kernels, work(): pl.pallas_call(functools.partial(work_kernel, batch), out_shape=[frame_sh...  23.3 us

profile of v2, /device:TPU:1, one launch (start us, length us, event | category | flops | bytes accessed | tf_op | source)
XLA Modules:
  0.0 155.7 jit_solution(9913086364491225805)
XLA Ops:
  0.6 1.3 copy.16.offsets
  2.0 25.7 %shard_map.138.frame.old = f32[2,4,512,128]{3,2,1,0:T(8,128)} custom-call(f32[256,256]{1,0:T(8,128)} %re_ref.1, f32[256,256]{1,0:T(8,128)} %im_ref.1), custom_call_target="tpu_custom_call" | custom-call | tf_op jit(solution)/shard_map/pallas_call | solution.py:759
  27.7 11.5 %shard_map.139 = (f32[2,4,512,128]{3,2,1,0:T(8,128)}, f32[2,2,256,256]{3,2,1,0:T(8,128)}) custom-call(s32[8]{0:T(128)} %bitcast.12, s32[8,2]{1,0:T(8,128)} %copy.16.offsets, f32[2,4,512,128]{3,2,1,0:T(8,128)} %shard_map.138.frame.old, f32[2,256,256]{2,1,0:T(8,128)} %probe_re.3, f32[2,256,256]{2,1,0:T(8,128)} %probe_im.3, f32[8,256,256]{2,1,0:T(8,128)} %bitcast.10, ...), custom_call_target="tpu_custom_call" | custom-call | flops 4300000256 | bytes 10000000 | tf_op jit(solution)/shard_map/pallas_call | solution.py:743
  39.3 48.8 %shard_map.140.frame.old = f32[2,4,512,128]{3,2,1,0:T(8,128)} custom-call(f32[2,4,512,128]{3,2,1,0:T(8,128)} %get-tuple-element.11.accum, f32[2,4,512,128]{3,2,1,0:T(8,128)} %shard_map.138.frame.old), custom_call_target="tpu_custom_call" | custom-call | tf_op jit(solution)/shard_map/pallas_call | solution.py:761
  88.0 11.8 %shard_map.141 = (f32[2,4,512,128]{3,2,1,0:T(8,128)}, f32[2,2,256,256]{3,2,1,0:T(8,128)}) custom-call(s32[8]{0:T(128)} %bitcast.13, s32[8,2]{1,0:T(8,128)} %copy.16.offsets, f32[2,4,512,128]{3,2,1,0:T(8,128)} %shard_map.140.frame.old, f32[2,256,256]{2,1,0:T(8,128)} %probe_re.3, f32[2,256,256]{2,1,0:T(8,128)} %probe_im.3, f32[8,256,256]{2,1,0:T(8,128)} %bitcast.11, ...), custom_call_target="tpu_custom_call" | custom-call | flops 4300000256 | bytes 10000000 | tf_op jit(solution)/shard_map/pallas_call | solution.py:743
  99.8 53.2 %shard_map.142 = (f32[256,256]{1,0:T(8,128)}, f32[256,256]{1,0:T(8,128)}, f32[1024,256]{1,0:T(8,128)}) custom-call(f32[2,4,512,128]{3,2,1,0:T(8,128)} %get-tuple-element.13.accum, f32[2,4,512,128]{3,2,1,0:T(8,128)} %shard_map.140.frame.old, f32[1024,256]{1,0:T(8,128)} %bitcast.6, f32[512,256]{1,0:T(8,128)} %bitcast.7, f32[512,256]{1,0:T(8,128)} %bitcast.8), custom_call_target="tpu_custom_call" | custom-call | tf_op jit(solution)/shard_map/pallas_call | solution.py:764
  153.1 2.6 %shard_map.143 = (f32[256,256]{1,0:T(8,128)}, f32[256,256]{1,0:T(8,128)}, f32[2,256,256]{2,1,0:T(8,128)}, f32[2,256,256]{2,1,0:T(8,128)}) custom-call(f32[256,256]{1,0:T(8,128)} %get-tuple-element.15.a, f32[256,256]{1,0:T(8,128)} %get-tuple-element.16.b, f32[1024,256]{1,0:T(8,128)} %get-tuple-element.17.flat), custom_call_target="tpu_custom_call" | custom-call | tf_op jit(solution)/shard_map/pallas_call | solution.py:791

commit v3 on v2

--- a/solution.py
+++ b/solution.py
@@ -1,4 +1,3 @@
-import functools
 import math
 
 import numpy as np
@@ -44,10 +43,8 @@
 def dft_operands():
     re, im = table(F)
     left = np.block([[re, -im], [im, re]])
-    back_left = np.block([[re, im], [-im, re]])
     right = np.block([[re, im], [-im, re]])
-    back_right = np.block([[re, -im], [im, re]])
-    return [jnp.asarray(m, jnp.float32).astype(jnp.bfloat16) for m in (left, back_left, right, back_right)]
+    return [jnp.asarray(m, jnp.float32).astype(jnp.bfloat16) for m in (left, right)]
 
 
 def part(pair):
@@ -58,7 +55,7 @@
     return (row >= 0) & (row < ROWS) & (col >= 0) & (col < COLS)
 
 
-def greet(peers):
+def greet(peers, meanwhile):
     barrier = pltpu.get_barrier_semaphore()
     count = jnp.int32(0)
     for there, device in peers:
@@ -68,6 +65,7 @@
             pl.semaphore_signal(barrier, inc=1, device_id=device, device_id_type=MESH)
 
         count = count + there.astype(jnp.int32)
+    meanwhile()
     pl.semaphore_wait(barrier, count)
 
 
@@ -312,20 +310,6 @@
         self.relay.wait_send()
 
 
-def halo_kernel(re_ref, im_ref, frame, held, *sems):
-    spot = Spot()
-    for channel, source in enumerate((re_ref, im_ref)):
-        for n in range(2):
-            frame[channel, 1 + n, H : H + F] = source[:, n * H : (n + 1) * H]
-    greet(spot.peers())
-    halo = Halo(spot, frame, held, *pairs(sems))
-    halo.begin(0)
-    halo.begin(1)
-    halo.aside()
-    clear_edges(spot.row, spot.col, frame)
-    halo.end()
-
-
 def pairs(sems):
     return [(sems[i], sems[i + 1]) for i in range(0, len(sems), 2)]
 
@@ -439,19 +423,13 @@
         self.relay.wait_send()
 
 
-def mid_kernel(accum, old, frame, cbuf, mbuf, vbuf, fbuf, stack, held, held2, *sems):
-    spot = Spot()
-    greet(spot.peers())
-    sems = pairs(sems)
-    fold = Fold(spot, accum, cbuf, mbuf, vbuf, fbuf, stack, held, *sems[:6])
-    halo = Halo(spot, frame, held2, *sems[6:])
+def renew(spot, fold, halo, accum, frame):
     fold.begin()
     fold.aside()
     fold.turn(0)
     fold.turn(1)
     fold.relay.turn()
-    clear_edges(spot.row, spot.col, frame)
-    frame[:, 1:3, H : H + F] = old[:, 1:3, H : H + F] + accum[:, 1:3, H : H + F]
+    frame[:, 1:3, H : H + F] = frame[:, 1:3, H : H + F] + accum[:, 1:3, H : H + F]
     for ch in range(2):
 
         def add(buf, rows, planes):
@@ -492,10 +470,7 @@
 COLORS = (("x", "y"), ("y", "x"))
 
 
-def last_kernel(accum, old, g, probe_re, probe_im, out_re, out_im, out, cbuf, mbuf, vbuf, fbuf, stack, held, *rest):
-    exchange, rest = rest[:12], rest[12:]
-    r0, w0, r1, w1, r2, w2, r3, w4, s0, q0, s1, q1, s2, q2, s3, q3, s4, q4, s5, q5, s6, q6 = rest
-    spot = Spot()
+def torus():
     sy, sx = lax.axis_index("sy"), lax.axis_index("sx")
     here = {
         "y": lax.div(sy, 4),
@@ -504,7 +479,6 @@
         "core": lax.rem(sx, 2),
     }
     size = {"x": 4, "y": 4, "z": 8, "core": 2}
-    rate = PROBE_GAIN / (8 * math.sqrt(ROWS * COLS))
 
     def place(axis, step):
         there = dict(here)
@@ -515,19 +489,20 @@
         )
         return there[axis], device
 
+    return here, place
+
+
+def finish_all(fold, accum, old, g, probe_re, probe_im, out_re, out_im, out, *rest):
+    r0, w0, r1, w1, r2, w2, r3, w4, s0, q0, s1, q1, s2, q2, s3, q3, s4, q4, s5, q5, s6, q6 = rest
+    here, place = torus()
+    rate = PROBE_GAIN / (8 * math.sqrt(ROWS * COLS))
+
     def send(src, dst, ss, rs, device):
         copy = pltpu.make_async_remote_copy(
             src_ref=src, dst_ref=dst, send_sem=ss, recv_sem=rs, device_id=device, device_id_type=MESH
         )
         copy.start()
         return copy
-
-    fold = Fold(spot, accum, cbuf, mbuf, vbuf, fbuf, stack, held, *pairs(exchange))
-    yes = sy >= 0
-    greet(
-        spot.peers()
-        + [(yes, place(axis, step)[1]) for axis in ("core", "x", "y", "z") for step in range(1, size[axis])]
-    )
 
     core = here["core"]
     other, partner = place("core", 1)
@@ -583,8 +558,9 @@
     for c, (first, second) in enumerate(COLORS):
         total = ((r3[c, 0] + r3[c, 1]) + (r3[c, 2] + r3[c, 3])) + ((r3[c, 4] + r3[c, 5]) + (r3[c, 6] + r3[c, 7]))
         start = c * 256 + here[first] * CHUNK1 + here[second] * CHUNK2
-        spots = pl.ds(pl.multiple_of(start, CHUNK2), CHUNK2)
-        base = jnp.where(core == 0, probe_re[spots], probe_im[spots])
+        own = pl.ds(pl.multiple_of(lax.rem(start, F), CHUNK2), CHUNK2)
+        mode = lax.div(start, F)
+        base = jnp.where(core == 0, probe_re[mode, own], probe_im[mode, own])
         w4[c, pl.ds(pl.multiple_of(here[second] * CHUNK2, CHUNK2), CHUNK2)] = base + rate * total
 
     copies = []
@@ -628,27 +604,20 @@
         out_d[m] = flat[(2 + m) * F : (3 + m) * F]
 
 
-def work_kernel(batch, order, offsets, frame, probe_re, probe_im, amps, left, back_left, right, back_right, *rest):
-    if batch == 0:
-        accum, grad, patch, fields, halves, amp, amp_sem = rest
-        grad_in = None
-    else:
-        grad_in, accum, grad, patch, fields, halves, amp, amp_sem = rest
+def place_terms(batch, order, offsets, accum, padded):
+    starts = []
+    for j in range(4):
+        starts.append(F - (offsets[order[batch * 4 + j], 0] + H))
+    for ch in range(2):
+        for n in range(4):
+            for row in range(0, E, H):
+                parts = [padded[j, ch, n, pl.ds(starts[j] + row, H), :] for j in range(4)]
+                accum[ch, n, row : row + H, :] = (parts[0] + parts[1]) + (parts[2] + parts[3])
+
+
+def work(batch, order, offsets, frame, probe_re, probe_im, amps, amp_ready, left, right, accum, grad, scale, padded, patch, fields, halves):
+    back_left, back_right = right, left
     size = 4
-    loads = []
-    for j in range(size):
-        p = order[batch * size + j]
-        load = pltpu.make_async_copy(amps.at[p], amp.at[j], amp_sem.at[j])
-        load.start()
-        loads.append(load)
-
-    power = jnp.max(
-        probe_re[0] * probe_re[0]
-        + probe_im[0] * probe_im[0]
-        + (probe_re[1] * probe_re[1] + probe_im[1] * probe_im[1])
-    )
-    scale = OBJECT_RATE / jnp.full((8, 128), power, jnp.float32)[0:1, 0:1]
-    accum[...] = jnp.zeros_like(accum)
     for j in range(size):
         p = order[batch * size + j]
         top = offsets[p, 0] + H
@@ -669,8 +638,9 @@
         far = jnp.dot(halves[2 * j * F : 2 * (j + 1) * F, :], right[...], preferred_element_type=jnp.float32)
         squares = far * far
         intensity = (squares[0:F, 0:F] + squares[0:F, F:]) + (squares[F:, 0:F] + squares[F:, F:])
-        loads[j].wait()
-        ratio = amp[j] * lax.rsqrt(jnp.maximum(intensity, 1.0))
+        if j == 0:
+            amp_ready()
+        ratio = amps[order[batch * size + j]] * lax.rsqrt(jnp.maximum(intensity, 1.0))
         for m in range(2):
             at = (2 * j + m) * F
             fields[2 * F : 3 * F, at : at + F] = (far[m * F : (m + 1) * F, 0:F] * ratio).astype(jnp.bfloat16)
@@ -699,73 +669,106 @@
             else:
                 terms = [terms[0] + o_re, terms[1] + o_im]
             for ch, g in enumerate((g_re, g_im)):
-                if j == 0:
-                    grad[ch, m] = g if grad_in is None else grad_in[ch, m] + g
+                own = pl.ds((2 * ch + m) * F, F)
+                if j == 0 and batch == 0:
+                    grad[own] = g
                 else:
-                    grad[ch, m] = grad[ch, m] + g
+                    grad[own] = grad[own] + g
         for ch in range(2):
-            wide = jnp.concatenate([terms[ch] * scale, jnp.zeros((F, F), jnp.float32)], axis=1)
+            wide = jnp.concatenate([terms[ch] * scale[0:1, 0:1], jnp.zeros((F, F), jnp.float32)], axis=1)
             wide = pltpu.roll(wide, shift, 1)
             for n in range(4):
-                accum[ch, n, pl.ds(top, F), :] += wide[:, n * H : (n + 1) * H]
+                padded[j, ch, n, F : 2 * F, :] = wide[:, n * H : (n + 1) * H]
+    place_terms(batch, order, offsets, accum, padded)
+
+
+def whole_kernel(order, offsets, re_ref, im_ref, probe_re_in, probe_im_in, amps_in, left_in, right_in, out_re, out_im, out, *scratch):
+    frame, accum, probe_re, probe_im, amps, left, right, grad, scale, padded, patch, fields, halves, load_sem = scratch[:14]
+    buffers, sems, rest = scratch[14:28], pairs(scratch[28:76]), scratch[76:]
+    spot = Spot()
+    loads = [
+        pltpu.make_async_copy(source, target, load_sem.at[i])
+        for i, (source, target) in enumerate(
+            [(probe_re_in, probe_re), (probe_im_in, probe_im), (left_in, left), (right_in, right), (amps_in, amps)]
+        )
+    ]
+    for load in loads:
+        load.start()
+
+    def meanwhile():
+        for channel, source in enumerate((re_ref, im_ref)):
+            for n in range(2):
+                frame[channel, 1 + n, H : H + F] = source[:, n * H : (n + 1) * H]
+        clear_edges(spot.row, spot.col, frame)
+
+    here, place = torus()
+    yes = spot.row >= 0
+    size = {"core": 2, "x": 4, "y": 4, "z": 8}
+    greet(
+        spot.peers()
+        + [(yes, place(axis, step)[1]) for axis in size for step in range(1, size[axis])],
+        meanwhile,
+    )
+    halo = Halo(spot, frame, buffers[12], *sems[0:6])
+    halo.begin(0)
+    halo.begin(1)
+    halo.aside()
+    blank = jnp.zeros((F, H), jnp.float32)
+    for j in range(4):
+        for ch in range(2):
+            for n in range(4):
+                padded[j, ch, n, 0:F] = blank
+                padded[j, ch, n, 2 * F : 3 * F] = blank
+    for load in loads[:4]:
+        load.wait()
+    power = jnp.max(
+        probe_re[0] * probe_re[0]
+        + probe_im[0] * probe_im[0]
+        + (probe_re[1] * probe_re[1] + probe_im[1] * probe_im[1]),
+        keepdims=True,
+    )
+    scale[...] = jnp.broadcast_to(OBJECT_RATE / power, (8, H))
+    halo.end()
+    common = (left, right, accum, grad, scale, padded, patch, fields, halves)
+    work(0, order, offsets, frame, probe_re, probe_im, amps, loads[4].wait, *common)
+    fold = Fold(spot, accum, *buffers[0:6], *sems[6:12])
+    halo = Halo(spot, frame, buffers[13], *sems[12:18])
+    renew(spot, fold, halo, accum, frame)
+    work(1, order, offsets, frame, probe_re, probe_im, amps, lambda: None, *common)
+    fold = Fold(spot, accum, *buffers[6:12], *sems[18:24])
+    finish_all(fold, accum, frame, grad, probe_re, probe_im, out_re, out_im, out, *rest)
 
 
 def local(object_re, object_im, probe_re, probe_im, amplitudes, offsets, visit_order):
-    f32 = jnp.float32
-    amps = amplitudes.reshape(8, F, F)
-    offs = offsets.reshape(8, 2)
-    order = visit_order.reshape(8)
-    tables = dft_operands()
-    frame_shape = jax.ShapeDtypeStruct((2, 4, E, H), f32)
-    grad_shape = jax.ShapeDtypeStruct((2, 2, F, F), f32)
-    limit = 60 * 1024 * 1024
-
-    def comm(kernel, outs, scratch, ident, n_in):
-        return pl.pallas_call(
-            kernel,
-            out_shape=outs,
-            in_specs=[VMEM] * n_in,
-            out_specs=[VMEM] * len(outs) if isinstance(outs, list) else VMEM,
-            scratch_shapes=scratch,
-            compiler_params=pltpu.CompilerParams(
-                collective_id=ident, has_side_effects=True, vmem_limit_bytes=limit
-            ),
-        )
-
+    f32, bf16 = jnp.float32, jnp.bfloat16
+    left, right = dft_operands()
     dma = pltpu.SemaphoreType.DMA
-
-    def work(batch, frame, grad):
-        ins = [order, offs, frame, probe_re, probe_im, amps, *tables]
-        specs = [SMEM, SMEM, VMEM, VMEM, VMEM, ANY] + [VMEM] * 4
-        if grad is not None:
-            ins.append(grad)
-            specs.append(VMEM)
-        return pl.pallas_call(
-            functools.partial(work_kernel, batch),
-            out_shape=[frame_shape, grad_shape],
-            in_specs=specs,
-            out_specs=[VMEM, VMEM],
-            scratch_shapes=[
-                pltpu.VMEM((4, 2, F, F), f32),
-                pltpu.VMEM((4 * F, 8 * F), jnp.bfloat16),
-                pltpu.VMEM((8 * F, 2 * F), jnp.bfloat16),
-                pltpu.VMEM((4, F, F), f32),
-                dma((4,)),
-            ],
-            compiler_params=pltpu.CompilerParams(vmem_limit_bytes=limit),
-            cost_estimate=pl.CostEstimate(flops=4_300_000_000, bytes_accessed=10_000_000, transcendentals=262144),
-        )(*ins)
-
-    frame = comm(halo_kernel, frame_shape, [held_buffer()] + exchange_sems(), 0, 2)(object_re, object_im)
-    accum, grad = work(0, frame, None)
-    frame = comm(mid_kernel, frame_shape, fold_buffers() + [held_buffer()] + exchange_sems() + exchange_sems(), 1, 2)(accum, frame)
-    accum, grad = work(1, frame, grad)
     tile_shape = jax.ShapeDtypeStruct((F, F), f32)
-    out_re, out_im, flat = comm(
-        last_kernel,
-        [tile_shape, tile_shape, jax.ShapeDtypeStruct((1024, F), f32)],
-        fold_buffers()
-        + exchange_sems()
+    out_re, out_im, flat = pl.pallas_call(
+        whole_kernel,
+        out_shape=[tile_shape, tile_shape, jax.ShapeDtypeStruct((4 * F, F), f32)],
+        in_specs=[SMEM, SMEM, VMEM, VMEM, ANY, ANY, ANY, ANY, ANY],
+        out_specs=[VMEM] * 3,
+        scratch_shapes=[
+            pltpu.VMEM((2, 4, E, H), f32),
+            pltpu.VMEM((2, 4, E, H), f32),
+            pltpu.VMEM((2, F, F), f32),
+            pltpu.VMEM((2, F, F), f32),
+            pltpu.VMEM((8, F, F), f32),
+            pltpu.VMEM((2 * F, 2 * F), bf16),
+            pltpu.VMEM((2 * F, 2 * F), bf16),
+            pltpu.VMEM((4 * F, F), f32),
+            pltpu.VMEM((8, H), f32),
+            pltpu.VMEM((4, 2, 4, 3 * F, H), f32),
+            pltpu.VMEM((4, 2, F, F), f32),
+            pltpu.VMEM((4 * F, 8 * F), bf16),
+            pltpu.VMEM((8 * F, 2 * F), bf16),
+            dma((5,)),
+        ]
+        + fold_buffers()
+        + fold_buffers()
+        + [held_buffer(), held_buffer()]
+        + exchange_sems() * 4
         + [
             pltpu.VMEM((512, F), f32),
             pltpu.VMEM((512, F), f32),
@@ -783,9 +786,20 @@
             dma((2, 3)), dma((2, 3)),
             dma, dma,
         ],
-        2,
-        5,
-    )(accum, frame, grad.reshape(1024, F), probe_re.reshape(512, F), probe_im.reshape(512, F))
+        compiler_params=pltpu.CompilerParams(
+            collective_id=0, has_side_effects=True, vmem_limit_bytes=62 * 1024 * 1024
+        ),
+    )(
+        visit_order.reshape(8),
+        offsets.reshape(8, 2),
+        object_re,
+        object_im,
+        probe_re,
+        probe_im,
+        amplitudes.reshape(8, F, F),
+        left,
+        right,
+    )
     probe_shape = jax.ShapeDtypeStruct((2, F, F), f32)
     return tuple(
         pl.pallas_call(

time: 156 us -> 125 us (0.80)
  Pallas kernels: 154 us -> 123 us
    pallas_call x5 -> x1, Pallas kernels: 151 us -> 121 us  [local(): pl.pallas_call(whole_kernel, out_shape=[tile_shape, tile_shape, jax.Shape...]
where the time goes in v3:
time: 125 us
  Pallas kernels  123 us (98%)
  local copies, waits for them, and re-layouts  1.35 us (1%)
    pallas_call x1, Pallas kernels, local(): pl.pallas_call(whole_kernel, out_shape=[tile_shape, tile_shape, jax.Shape...  121 us
    pallas_call x1, Pallas kernels, local(): pl.pallas_call(write_kernel, out_shape=[tile_shape, tile_shape, probe_sha...  2.55 us

profile of v3, /device:TPU:1, one launch (start us, length us, event | category | flops | bytes accessed | tf_op | source)
XLA Modules:
  0.0 125.1 jit_solution(16686379241793703609)
XLA Ops:
  0.6 1.3 %copy.13.offsets = s32[8,2]{1,0:T(8,128)} copy(s32[8,2]{0,1:T(2,128)} %bitcast.4) | data formatting | bytes 128 | tf_op jit(solution)/shard_map/reshape | solution.py:794
  2.0 120.6 %shard_map.120 = (f32[256,256]{1,0:T(8,128)}, f32[256,256]{1,0:T(8,128)}, f32[1024,256]{1,0:T(8,128)}) custom-call(s32[8]{0:T(128)} %bitcast.5, s32[8,2]{1,0:T(8,128)} %copy.13.offsets, f32[256,256]{1,0:T(8,128)} %re_ref.1, f32[256,256]{1,0:T(8,128)} %im_ref.1, f32[2,256,256]{2,1,0:T(8,128)} %probe_re_in.1, f32[2,256,256]{2,1,0:T(8,128)} %probe_im_in.1, ...), custom_call_target="tpu_custom_call" | custom-call | tf_op jit(solution)/shard_map/pallas_call | solution.py:747
  122.6 2.6 %shard_map.121 = (f32[256,256]{1,0:T(8,128)}, f32[256,256]{1,0:T(8,128)}, f32[2,256,256]{2,1,0:T(8,128)}, f32[2,256,256]{2,1,0:T(8,128)}) custom-call(f32[256,256]{1,0:T(8,128)} %get-tuple-element.7.a, f32[256,256]{1,0:T(8,128)} %get-tuple-element.8.b, f32[1024,256]{1,0:T(8,128)} %get-tuple-element.9.flat), custom_call_target="tpu_custom_call" | custom-call | tf_op jit(solution)/shard_map/pallas_call | solution.py:805

commit v4 on v3

--- a/solution.py
+++ b/solution.py
@@ -423,8 +423,10 @@
         self.relay.wait_send()
 
 
-def renew(spot, fold, halo, accum, frame):
-    fold.begin()
+def renew(spot, fold, halo, accum, frame, place_channel):
+    for ch in range(2):
+        place_channel(ch)
+        fold.corners[ch].start()
     fold.aside()
     fold.turn(0)
     fold.turn(1)
@@ -492,10 +494,14 @@
     return here, place
 
 
-def finish_all(fold, accum, old, g, probe_re, probe_im, out_re, out_im, out, *rest):
+def finish_all(fold, place_channel, accum, old, g, probe_re, probe_im, out_re, out_im, out, *rest):
     r0, w0, r1, w1, r2, w2, r3, w4, s0, q0, s1, q1, s2, q2, s3, q3, s4, q4, s5, q5, s6, q6 = rest
     here, place = torus()
     rate = PROBE_GAIN / (8 * math.sqrt(ROWS * COLS))
+    core = here["core"]
+    other, partner = place("core", 1)
+    mine = pl.ds(pl.multiple_of(core * 512, 512), 512)
+    theirs = pl.ds(pl.multiple_of(other * 512, 512), 512)
 
     def send(src, dst, ss, rs, device):
         copy = pltpu.make_async_remote_copy(
@@ -504,47 +510,46 @@
         copy.start()
         return copy
 
-    core = here["core"]
-    other, partner = place("core", 1)
-    mine = pl.ds(pl.multiple_of(core * 512, 512), 512)
-    theirs = pl.ds(pl.multiple_of(other * 512, 512), 512)
-    first_copy = send(g.at[theirs], r0, s0, q0, partner)
-    first_copy.wait()
+    def rows(start, count):
+        return pl.ds(pl.multiple_of(start, count), count)
+
+    def wait(copies):
+        for copy in copies:
+            copy.wait()
+
+    across_cores = send(g.at[theirs], r0, s0, q0, partner)
+    place_channel(0)
+    place_channel(1)
+    across_cores.wait()
     w0[...] = g[mine] + r0[...]
 
     copies = []
     for c, (first, second) in enumerate(COLORS):
+        copies.append([])
         for step in (1, 2, 3):
             index, device = place(first, step)
-            source = w0.at[pl.ds(pl.multiple_of(c * 256 + index * CHUNK1, CHUNK1), CHUNK1)]
-            copies.append(send(source, r1.at[c, step - 1], s1.at[c, step - 1], q1.at[c, step - 1], device))
+            source = w0.at[rows(c * 256 + index * CHUNK1, CHUNK1)]
+            copies[c].append(send(source, r1.at[c, step - 1], s1.at[c, step - 1], q1.at[c, step - 1], device))
     fold.begin()
-    for copy in copies:
-        copy.wait()
     for c, (first, second) in enumerate(COLORS):
-        own = w0[pl.ds(pl.multiple_of(c * 256 + here[first] * CHUNK1, CHUNK1), CHUNK1)]
+        wait(copies[c])
+        own = w0[rows(c * 256 + here[first] * CHUNK1, CHUNK1)]
         w1[c] = (own + r1[c, 0]) + (r1[c, 1] + r1[c, 2])
-
-    copies = []
-    for c, (first, second) in enumerate(COLORS):
+        copies[c] = []
         for step in (1, 2, 3):
             index, device = place(second, step)
-            source = w1.at[c, pl.ds(pl.multiple_of(index * CHUNK2, CHUNK2), CHUNK2)]
-            copies.append(send(source, r2.at[c, step - 1], s2.at[c, step - 1], q2.at[c, step - 1], device))
-    for copy in copies:
-        copy.wait()
+            source = w1.at[c, rows(index * CHUNK2, CHUNK2)]
+            copies[c].append(send(source, r2.at[c, step - 1], s2.at[c, step - 1], q2.at[c, step - 1], device))
+    fold.turn(0)
     for c, (first, second) in enumerate(COLORS):
-        own = w1[c, pl.ds(pl.multiple_of(here[second] * CHUNK2, CHUNK2), CHUNK2)]
+        wait(copies[c])
+        own = w1[c, rows(here[second] * CHUNK2, CHUNK2)]
         w2[c] = (own + r2[c, 0]) + (r2[c, 1] + r2[c, 2])
-
-    copies = []
-    for c in range(2):
+        copies[c] = []
         for step in range(1, 8):
-            index, device = place("z", step)
-            copies.append(send(w2.at[c], r3.at[c, here["z"]], s3.at[c, step - 1], q3.at[c, step - 1], device))
-    for c in range(2):
+            device = place("z", step)[1]
+            copies[c].append(send(w2.at[c], r3.at[c, here["z"]], s3.at[c, step - 1], q3.at[c, step - 1], device))
         r3[c, here["z"]] = w2[c]
-    fold.turn(0)
     fold.turn(1)
     fold.aside()
     fold.relay.turn()
@@ -552,76 +557,81 @@
     for channel, tile in enumerate(outs):
         for n in range(2):
             tile[:, n * H : (n + 1) * H] = old[channel, 1 + n, H : H + F] + accum[channel, 1 + n, H : H + F]
-
-    for copy in copies:
-        copy.wait()
     for c, (first, second) in enumerate(COLORS):
+        wait(copies[c])
         total = ((r3[c, 0] + r3[c, 1]) + (r3[c, 2] + r3[c, 3])) + ((r3[c, 4] + r3[c, 5]) + (r3[c, 6] + r3[c, 7]))
         start = c * 256 + here[first] * CHUNK1 + here[second] * CHUNK2
-        own = pl.ds(pl.multiple_of(lax.rem(start, F), CHUNK2), CHUNK2)
+        own = rows(lax.rem(start, F), CHUNK2)
         mode = lax.div(start, F)
         base = jnp.where(core == 0, probe_re[mode, own], probe_im[mode, own])
-        w4[c, pl.ds(pl.multiple_of(here[second] * CHUNK2, CHUNK2), CHUNK2)] = base + rate * total
-
-    copies = []
+        spot = rows(here[second] * CHUNK2, CHUNK2)
+        w4[c, spot] = base + rate * total
+        copies[c] = []
+        for step in (1, 2, 3):
+            device = place(second, step)[1]
+            copies[c].append(send(w4.at[c, spot], w4.at[c, spot], s4.at[c, step - 1], q4.at[c, step - 1], device))
+    last = []
     for c, (first, second) in enumerate(COLORS):
-        spot = w4.at[c, pl.ds(pl.multiple_of(here[second] * CHUNK2, CHUNK2), CHUNK2)]
+        wait(copies[c])
+        spot = out.at[rows(core * 512 + c * 256 + here[first] * CHUNK1, CHUNK1)]
+        copies[c] = []
         for step in (1, 2, 3):
-            copies.append(send(spot, spot, s4.at[c, step - 1], q4.at[c, step - 1], place(second, step)[1]))
-    for copy in copies:
-        copy.wait()
-
-    copies = []
+            device = place(first, step)[1]
+            copies[c].append(send(w4.at[c], spot, s5.at[c, step - 1], q5.at[c, step - 1], device))
+        out[rows(core * 512 + c * 256 + here[first] * CHUNK1, CHUNK1)] = w4[c]
+        last.append(send(w4.at[c], spot, s6.at[c, 0], q6.at[c, 0], partner))
+    for ch, tile in enumerate(outs):
+
+        def add(buf, where_rows, planes):
+            for n in range(planes[1]):
+                where = (pl.ds(where_rows[0] - H, where_rows[1]), pl.ds((planes[0] - 1 + n) * H, H))
+                tile[where] = tile[where] + buf[n]
+
+        fold.end(ch, add)
     for c, (first, second) in enumerate(COLORS):
-        start = core * 512 + c * 256 + here[first] * CHUNK1
-        spot = out.at[pl.ds(pl.multiple_of(start, CHUNK1), CHUNK1)]
         for step in (1, 2, 3):
-            copies.append(send(w4.at[c], spot, s5.at[c, step - 1], q5.at[c, step - 1], place(first, step)[1]))
-    for c, (first, second) in enumerate(COLORS):
-        start = core * 512 + c * 256 + here[first] * CHUNK1
-        out[pl.ds(pl.multiple_of(start, CHUNK1), CHUNK1)] = w4[c]
-    for copy in copies:
-        copy.wait()
-
-    last_copy = send(out.at[mine], out.at[mine], s6, q6, partner)
-    for ch, tile in enumerate(outs):
-
-        def add(buf, rows, planes):
-            for n in range(planes[1]):
-                where = (pl.ds(rows[0] - H, rows[1]), pl.ds((planes[0] - 1 + n) * H, H))
-                tile[where] = tile[where] + buf[n]
-
-        fold.end(ch, add)
+            copies[c][step - 1].wait()
+            source = place(first, 4 - step)[0]
+            spot = out.at[rows(core * 512 + c * 256 + source * CHUNK1, CHUNK1)]
+            last.append(send(spot, spot, s6.at[c, step], q6.at[c, step], partner))
     fold.close()
-    last_copy.wait()
-
-
-def write_kernel(a, b, flat, out_a, out_b, out_c, out_d):
-    out_a[...] = a[...]
-    out_b[...] = b[...]
-    for m in range(2):
-        out_c[m] = flat[m * F : (m + 1) * F]
-        out_d[m] = flat[(2 + m) * F : (3 + m) * F]
-
-
-def place_terms(batch, order, offsets, accum, padded):
+    wait(last)
+
+
+def write_kernel(a, b, flat, out_a, out_b, out_c, out_d, held_a, held_b, held_flat, load_sem, store_sem):
+    parts = [(a, held_a, out_a), (b, held_b, out_b)]
+    for k, out in enumerate((out_c, out_d)):
+        for m in range(2):
+            rows = pl.ds((2 * k + m) * F, F)
+            parts.append((flat.at[rows], held_flat.at[rows], out.at[m]))
+    loads = [pltpu.make_async_copy(src, held, load_sem.at[i]) for i, (src, held, _) in enumerate(parts)]
+    stores = [pltpu.make_async_copy(held, out, store_sem.at[i]) for i, (_, held, out) in enumerate(parts)]
+    for load in loads:
+        load.start()
+    for load, store in zip(loads, stores):
+        load.wait()
+        store.start()
+    for store in stores:
+        store.wait()
+
+
+def place_terms(ch, batch, order, offsets, accum, padded):
     starts = []
     for j in range(4):
-        starts.append(F - (offsets[order[batch * 4 + j], 0] + H))
-    for ch in range(2):
-        for n in range(4):
-            for row in range(0, E, H):
-                parts = [padded[j, ch, n, pl.ds(starts[j] + row, H), :] for j in range(4)]
-                accum[ch, n, row : row + H, :] = (parts[0] + parts[1]) + (parts[2] + parts[3])
+        starts.append(F - (offsets[0, 0, 0, order[0, 0, batch * 4 + j]] + H))
+    for n in range(4):
+        for row in range(0, E, H):
+            parts = [padded[j, ch, n, pl.ds(starts[j] + row, H), :] for j in range(4)]
+            accum[ch, n, row : row + H, :] = (parts[0] + parts[1]) + (parts[2] + parts[3])
 
 
 def work(batch, order, offsets, frame, probe_re, probe_im, amps, amp_ready, left, right, accum, grad, scale, padded, patch, fields, halves):
     back_left, back_right = right, left
     size = 4
     for j in range(size):
-        p = order[batch * size + j]
-        top = offsets[p, 0] + H
-        shift = offsets[p, 1] + H
+        p = order[0, 0, batch * size + j]
+        top = offsets[0, 0, 0, p] + H
+        shift = offsets[0, 0, 1, p] + H
         for ch in range(2):
             rows = jnp.concatenate([frame[ch, n, pl.ds(top, F), :] for n in range(4)], axis=1)
             patch[j, ch] = pltpu.roll(rows, lax.rem(E - shift, E), 1)[:, :F]
@@ -640,7 +650,7 @@
         intensity = (squares[0:F, 0:F] + squares[0:F, F:]) + (squares[F:, 0:F] + squares[F:, F:])
         if j == 0:
             amp_ready()
-        ratio = amps[order[batch * size + j]] * lax.rsqrt(jnp.maximum(intensity, 1.0))
+        ratio = amps[order[0, 0, batch * size + j]] * lax.rsqrt(jnp.maximum(intensity, 1.0))
         for m in range(2):
             at = (2 * j + m) * F
             fields[2 * F : 3 * F, at : at + F] = (far[m * F : (m + 1) * F, 0:F] * ratio).astype(jnp.bfloat16)
@@ -650,9 +660,9 @@
         halves[n * F : (n + 1) * F, 0:F] = half[0:F].astype(jnp.bfloat16)
         halves[n * F : (n + 1) * F, F : 2 * F] = half[F:].astype(jnp.bfloat16)
     for j in range(size):
-        p = order[batch * size + j]
-        top = offsets[p, 0] + H
-        shift = offsets[p, 1] + H
+        p = order[0, 0, batch * size + j]
+        top = offsets[0, 0, 0, p] + H
+        shift = offsets[0, 0, 1, p] + H
         back = jnp.dot(halves[2 * j * F : 2 * (j + 1) * F, :], back_right[...], preferred_element_type=jnp.float32)
         re, im = patch[j, 0], patch[j, 1]
         terms = [None, None]
@@ -679,7 +689,6 @@
             wide = pltpu.roll(wide, shift, 1)
             for n in range(4):
                 padded[j, ch, n, F : 2 * F, :] = wide[:, n * H : (n + 1) * H]
-    place_terms(batch, order, offsets, accum, padded)
 
 
 def whole_kernel(order, offsets, re_ref, im_ref, probe_re_in, probe_im_in, amps_in, left_in, right_in, out_re, out_im, out, *scratch):
@@ -733,10 +742,10 @@
     work(0, order, offsets, frame, probe_re, probe_im, amps, loads[4].wait, *common)
     fold = Fold(spot, accum, *buffers[0:6], *sems[6:12])
     halo = Halo(spot, frame, buffers[13], *sems[12:18])
-    renew(spot, fold, halo, accum, frame)
+    renew(spot, fold, halo, accum, frame, lambda ch: place_terms(ch, 0, order, offsets, accum, padded))
     work(1, order, offsets, frame, probe_re, probe_im, amps, lambda: None, *common)
     fold = Fold(spot, accum, *buffers[6:12], *sems[18:24])
-    finish_all(fold, accum, frame, grad, probe_re, probe_im, out_re, out_im, out, *rest)
+    finish_all(fold, lambda ch: place_terms(ch, 1, order, offsets, accum, padded), accum, frame, grad, probe_re, probe_im, out_re, out_im, out, *rest)
 
 
 def local(object_re, object_im, probe_re, probe_im, amplitudes, offsets, visit_order):
@@ -784,14 +793,14 @@
             dma((2, 7)), dma((2, 7)),
             dma((2, 3)), dma((2, 3)),
             dma((2, 3)), dma((2, 3)),
-            dma, dma,
+            dma((2, 4)), dma((2, 4)),
         ],
         compiler_params=pltpu.CompilerParams(
             collective_id=0, has_side_effects=True, vmem_limit_bytes=62 * 1024 * 1024
         ),
     )(
-        visit_order.reshape(8),
-        offsets.reshape(8, 2),
+        visit_order,
+        jnp.swapaxes(offsets, 2, 3),
         object_re,
         object_im,
         probe_re,
@@ -805,8 +814,15 @@
         pl.pallas_call(
             write_kernel,
             out_shape=[tile_shape, tile_shape, probe_shape, probe_shape],
-            in_specs=[VMEM] * 3,
-            out_specs=[VMEM] * 4,
+            in_specs=[ANY] * 3,
+            out_specs=[ANY] * 4,
+            scratch_shapes=[
+                pltpu.VMEM((F, F), f32),
+                pltpu.VMEM((F, F), f32),
+                pltpu.VMEM((4 * F, F), f32),
+                dma((6,)),
+                dma((6,)),
+            ],
         )(out_re, out_im, flat)
     )
 

time: 125 us -> 123 us (0.984)
  local copies, waits for them, and re-layouts: 1.35 us -> 0 us
    reshape x1 -> x0, local copies, waits for them, and re-layouts: 1.35 us -> none  [local(): offsets.reshape(8, 2)]
where the time goes in v4:
time: 123 us
  Pallas kernels  123 us (100%)
    pallas_call x1, Pallas kernels, local(): pl.pallas_call(whole_kernel, out_shape=[tile_shape, tile_shape, jax.Shape...  120 us

profile of v4, /device:TPU:1, one launch (start us, length us, event | category | flops | bytes accessed | tf_op | source)
XLA Modules:
  0.0 123.4 jit_solution(7845853101469514199)
XLA Ops:
  0.6 120.4 %shard_map.120 = (f32[256,256]{1,0:T(8,128)}, f32[256,256]{1,0:T(8,128)}, f32[1024,256]{1,0:T(8,128)}) custom-call(s32[1,1,8]{2,1,0:T(1,128)} %order.1, s32[1,1,2,8]{3,2,1,0:T(2,128)} %bitcast.3, f32[256,256]{1,0:T(8,128)} %re_ref.1, f32[256,256]{1,0:T(8,128)} %im_ref.1, f32[2,256,256]{2,1,0:T(8,128)} %probe_re_in.1, f32[2,256,256]{2,1,0:T(8,128)} %probe_im_in.1, ...), custom_call_target="tpu_custom_call" | custom-call | tf_op jit(solution)/shard_map/pallas_call | solution.py:756
  121.1 2.2 %shard_map.121 = (f32[256,256]{1,0:T(8,128)}, f32[256,256]{1,0:T(8,128)}, f32[2,256,256]{2,1,0:T(8,128)}, f32[2,256,256]{2,1,0:T(8,128)}) custom-call(f32[256,256]{1,0:T(8,128)} %get-tuple-element.7.a, f32[256,256]{1,0:T(8,128)} %get-tuple-element.8.b, f32[1024,256]{1,0:T(8,128)} %get-tuple-element.9.flat), custom_call_target="tpu_custom_call" | custom-call | tf_op jit(solution)/shard_map/pallas_call | solution.py:814

commit v5 on v4

--- a/solution.py
+++ b/solution.py
@@ -97,7 +97,16 @@
             (self.seam & (col != c) & (jnp.abs(col - c) != 1), (row, jnp.int32(c))) for c in range(COLS)
         ]
         edges = [(~self.seam & (jnp.abs(col - c) != 1), (row, jnp.int32(c))) for c in (SEAM - 1, SEAM)]
-        return near + diagonal + relays[: SEAM - 1] + relays[SEAM + 1 :] + [
+        slants = [
+            (self.has(dr, 0) & (self.half == 1 - half) & there, (row + dr, device[1]))
+            for half in (0, 1)
+            for dr in (-1, 1)
+            for there, device in (
+                [(self.col == SEAM - half, (row, jnp.int32(c))) for c in range(half * SEAM, half * SEAM + SEAM) if c not in (SEAM - 1, SEAM)]
+                + [(~self.seam, (row, jnp.int32(SEAM - 1 + half)))]
+            )
+        ]
+        return near + diagonal + slants + relays[: SEAM - 1] + relays[SEAM + 1 :] + [
             (self.seam & (there), device) for there, device in relays[SEAM - 1 : SEAM + 1]
         ] + edges
 
@@ -161,18 +170,20 @@
 
 
 FOUR = [(k, n) for k in range(2) for n in range(2)]
-SLICE = F // SEAM
+STRIPS = ((-1, H // SEAM), (1, H // SEAM), (0, F // SEAM))
 
 
 class Relay:
-    def __init__(self, spot, source, target, held, first, second):
+    def __init__(self, spot, dr, count, source, target, held, first, second):
         self.spot, self.source, self.target, self.held = spot, source, target, held
-        self.first, self.second = first, second
+        self.first, self.second, self.count = first, second, count
+        self.sends, self.gets = spot.has(dr, 0), spot.seam & spot.has(-dr, 0)
+        self.goal = (spot.row + dr, spot.beyond[1])
 
     def out(self, q):
         spot = self.spot
         device = (spot.row, spot.half * SEAM + q)
-        return remote(self.source(q * SLICE), self.held, self.first, q, device)
+        return remote(self.source(q * self.count), self.held, self.first, q, device)
 
     def arrive(self):
         return pltpu.make_async_remote_copy(
@@ -181,30 +192,30 @@
         )
 
     def on(self, q, src):
-        return remote(src, self.target(pl.multiple_of(q * SLICE, SLICE)), self.second, q, self.spot.beyond)
+        return remote(src, self.target(pl.multiple_of(q * self.count, self.count)), self.second, q, self.goal)
 
     def start(self):
         spot = self.spot
         for q in range(SEAM):
 
-            @pl.when(spot.seam & (spot.seat != q))
+            @pl.when(self.sends & spot.seam & (spot.seat != q))
             def _():
                 self.out(q).start()
 
         for half, q in ((0, SEAM - 1), (1, 0)):
 
-            @pl.when(spot.seam & (spot.half == half))
-            def _():
-                self.on(q, self.source(q * SLICE)).start()
+            @pl.when(self.sends & spot.seam & (spot.half == half))
+            def _():
+                self.on(q, self.source(q * self.count)).start()
 
     def turn(self):
-        @pl.when(~self.spot.seam)
+        @pl.when(self.sends & ~self.spot.seam)
         def _():
             self.arrive().wait_recv()
             self.on(self.spot.seat, self.held).start()
 
     def wait_recv(self):
-        @pl.when(self.spot.seam)
+        @pl.when(self.gets)
         def _():
             for q in range(SEAM):
                 self.on(q, self.held).wait_recv()
@@ -212,25 +223,25 @@
     def wait_send(self):
         spot = self.spot
 
-        @pl.when(~spot.seam)
+        @pl.when(self.sends & ~spot.seam)
         def _():
             self.on(spot.seat, self.held).wait_send()
 
         for q in range(SEAM):
 
-            @pl.when(spot.seam & (spot.seat != q))
+            @pl.when(self.sends & spot.seam & (spot.seat != q))
             def _():
                 self.out(q).wait_send()
 
         for half, q in ((0, SEAM - 1), (1, 0)):
 
-            @pl.when(spot.seam & (spot.half == half))
+            @pl.when(self.sends & spot.seam & (spot.half == half))
             def _():
                 self.on(q, self.held).wait_send()
 
 
 class Halo:
-    def __init__(self, spot, frame, held, upright, level, corner, seam, first, second):
+    def __init__(self, spot, frame, held, upright, level, corner, *relay_sems):
         self.spot, self.frame = spot, frame
 
         def strip(ch, dr, planes, rows_from, to_rows, to_planes, sems, k, device):
@@ -249,15 +260,6 @@
                 strip(ch, dr, (1, 2), TILE_ROWS[dr], FRAME_ROWS[dr], (1, 2), upright, k, spot.at(dr, 0)),
             )
             for k, dr in enumerate(SIDES)
-        ])
-        self.across = both(lambda ch: [
-            (
-                spot.has(dr, dc) & spot.far(dc),
-                spot.has(-dr, -dc) & spot.far(-dc),
-                strip(ch, dr, TILE_PLANES[dc], TILE_ROWS[dr], FRAME_ROWS[dr], FRAME_PLANES[dc], seam, 2 * k + n, spot.at(dr, dc)),
-            )
-            for k, dr in enumerate(SIDES)
-            for n, dc in enumerate(SIDES)
         ])
         self.middle = both(lambda ch: [
             (
@@ -277,22 +279,26 @@
             for n, dc in enumerate(SIDES)
         ])
         half = spot.half
-        self.relay = Relay(
-            spot,
-            lambda row: frame.at[:, pl.ds(2 - half, 1), pl.ds(H + row, SLICE)],
-            lambda row: frame.at[:, pl.ds(3 * half, 1), pl.ds(H + row, SLICE)],
-            held, first, second,
-        )
+        self.relays = [
+            Relay(
+                spot, dr, count,
+                lambda row, dr=dr, count=count: frame.at[:, pl.ds(2 - half, 1), pl.ds(TILE_ROWS[dr][0] + row, count)],
+                lambda row, dr=dr, count=count: frame.at[:, pl.ds(3 * half, 1), pl.ds(FRAME_ROWS[dr][0] + row, count)],
+                held[i], relay_sems[2 * i], relay_sems[2 * i + 1],
+            )
+            for i, (dr, count) in enumerate(STRIPS)
+        ]
 
     def begin(self, ch):
         self.vertical[ch].start()
-        self.across[ch].start()
 
     def aside(self):
-        self.relay.start()
+        for relay in self.relays:
+            relay.start()
         self.middle[0].start()
         self.middle[1].start()
-        self.relay.turn()
+        for relay in self.relays:
+            relay.turn()
 
     def end(self):
         for ch in range(2):
@@ -300,14 +306,15 @@
             self.corners[ch].start()
         for ch in range(2):
             self.middle[ch].wait_recv()
-        self.relay.wait_recv()
+        for relay in self.relays:
+            relay.wait_recv()
         for ch in range(2):
-            for transfers in (self.across[ch], self.corners[ch]):
-                transfers.wait_recv()
+            self.corners[ch].wait_recv()
         for ch in range(2):
-            for transfers in (self.vertical[ch], self.middle[ch], self.across[ch], self.corners[ch]):
+            for transfers in (self.vertical[ch], self.middle[ch], self.corners[ch]):
                 transfers.wait_send()
-        self.relay.wait_send()
+        for relay in self.relays:
+            relay.wait_send()
 
 
 def pairs(sems):
@@ -315,7 +322,7 @@
 
 
 class Fold:
-    def __init__(self, spot, accum, cbuf, mbuf, vbuf, fbuf, stack, held, upright, level, corner, seam, first, second):
+    def __init__(self, spot, accum, cbuf, mbuf, vbuf, fbuf, stack, held, upright, level, corner, *relay_sems):
         self.spot, self.accum, self.stack = spot, accum, stack
         self.cbuf, self.mbuf, self.vbuf, self.fbuf = cbuf, mbuf, vbuf, fbuf
 
@@ -332,15 +339,6 @@
                 strip(ch, OUTER_PLANES[dc], OUTER_ROWS[side], cbuf, corner, 2 * k + n, spot.at(0, dc)),
             )
             for k, side in enumerate(SIDES)
-            for n, dc in enumerate(SIDES)
-        ])
-        self.across = both(lambda ch: [
-            (
-                spot.has(dr, dc) & spot.far(dc),
-                spot.has(-dr, -dc) & spot.far(-dc),
-                strip(ch, OUTER_PLANES[dc], OUTER_ROWS[dr], fbuf, seam, 2 * k + n, spot.at(dr, dc)),
-            )
-            for k, dr in enumerate(SIDES)
             for n, dc in enumerate(SIDES)
         ])
         self.middle = both(lambda ch: [
@@ -360,21 +358,34 @@
             for k, dr in enumerate(SIDES)
         ])
         half = spot.half
-        self.relay = Relay(
-            spot,
-            lambda row: accum.at[:, pl.ds(3 - 3 * half, 1), pl.ds(H + row, SLICE)],
-            lambda row: mbuf.at[:, 1 - half, :, pl.ds(row, SLICE)],
-            held, first, second,
-        )
+        targets = {
+            -1: lambda row, count: fbuf.at[:, 1 - half, :, pl.ds(row, count)],
+            1: lambda row, count: fbuf.at[:, 3 - half, :, pl.ds(row, count)],
+            0: lambda row, count: mbuf.at[:, 1 - half, :, pl.ds(row, count)],
+        }
+        self.relays = [
+            Relay(
+                spot, dr, count,
+                lambda row, dr=dr, count=count: accum.at[:, pl.ds(3 - 3 * half, 1), pl.ds(OUTER_ROWS[dr][0] + row, count)],
+                lambda row, dr=dr, count=count: targets[dr](row, count),
+                held[i], relay_sems[2 * i], relay_sems[2 * i + 1],
+            )
+            for i, (dr, count) in enumerate(STRIPS)
+        ]
 
     def begin(self):
         self.corners[0].start()
         self.corners[1].start()
 
     def aside(self):
-        self.relay.start()
+        for relay in self.relays:
+            relay.start()
         self.middle[0].start()
         self.middle[1].start()
+
+    def pass_on(self):
+        for relay in self.relays:
+            relay.turn()
 
     def turn(self, ch):
         stack, cbuf = self.stack, self.cbuf
@@ -389,13 +400,13 @@
                 stack[ch, k, plane] = stack[ch, k, plane] + cbuf[ch, 2 * k + n, 0]
 
         self.vertical[ch].start()
-        self.across[ch].start()
 
     def end(self, ch, add):
         spot = self.spot
         self.middle[ch].wait_recv()
         if ch == 0:
-            self.relay.wait_recv()
+            for relay in self.relays:
+                relay.wait_recv()
         for n, dc in enumerate(SIDES):
 
             @pl.when(spot.has(0, -dc))
@@ -409,18 +420,19 @@
             def _():
                 add(self.vbuf.at[ch, k], INNER_ROWS[dr], (1, 2))
 
-        self.across[ch].wait_recv()
-        for (_, received, _), (k, n) in zip(self.across[ch].entries, FOUR):
-
-            @pl.when(received)
-            def _():
-                add(self.fbuf.at[ch, 2 * k + n], INNER_ROWS[SIDES[k]], INNER_PLANES[SIDES[n]])
+        for k, n in FOUR:
+            dr, dc = SIDES[k], SIDES[n]
+
+            @pl.when(spot.has(-dr, -dc) & spot.far(-dc))
+            def _():
+                add(self.fbuf.at[ch, 2 * k + n], INNER_ROWS[dr], INNER_PLANES[dc])
 
     def close(self):
         for ch in range(2):
-            for transfers in (self.corners[ch], self.across[ch], self.middle[ch], self.vertical[ch]):
+            for transfers in (self.corners[ch], self.middle[ch], self.vertical[ch]):
                 transfers.wait_send()
-        self.relay.wait_send()
+        for relay in self.relays:
+            relay.wait_send()
 
 
 def renew(spot, fold, halo, accum, frame, place_channel):
@@ -430,7 +442,7 @@
     fold.aside()
     fold.turn(0)
     fold.turn(1)
-    fold.relay.turn()
+    fold.pass_on()
     frame[:, 1:3, H : H + F] = frame[:, 1:3, H : H + F] + accum[:, 1:3, H : H + F]
     for ch in range(2):
 
@@ -445,8 +457,8 @@
     fold.close()
 
 
-def held_buffer():
-    return pltpu.VMEM((2, 1, SLICE, H), jnp.float32)
+def held_buffers():
+    return [pltpu.VMEM((2, 1, count, H), jnp.float32) for _, count in STRIPS]
 
 
 def fold_buffers():
@@ -457,13 +469,12 @@
         pltpu.VMEM((2, 2, 2, H, H), f32),
         pltpu.VMEM((2, 4, 1, H, H), f32),
         pltpu.VMEM((2, 2, 2, H, H), f32),
-        held_buffer(),
     ]
 
 
 def exchange_sems():
     dma = pltpu.SemaphoreType.DMA
-    shapes = ((2, 2), (2, 2), (2, 4), (2, 4), (SEAM,), (SEAM,))
+    shapes = ((2, 2), (2, 2), (2, 4)) + ((SEAM,),) * 6
     return [dma(shape) for shape in shapes for _ in range(2)]
 
 
@@ -552,7 +563,7 @@
         r3[c, here["z"]] = w2[c]
     fold.turn(1)
     fold.aside()
-    fold.relay.turn()
+    fold.pass_on()
     outs = (out_re, out_im)
     for channel, tile in enumerate(outs):
         for n in range(2):
@@ -693,7 +704,7 @@
 
 def whole_kernel(order, offsets, re_ref, im_ref, probe_re_in, probe_im_in, amps_in, left_in, right_in, out_re, out_im, out, *scratch):
     frame, accum, probe_re, probe_im, amps, left, right, grad, scale, padded, patch, fields, halves, load_sem = scratch[:14]
-    buffers, sems, rest = scratch[14:28], pairs(scratch[28:76]), scratch[76:]
+    buffers, held, sems, rest = scratch[14:24], scratch[24:36], pairs(scratch[36:108]), scratch[108:]
     spot = Spot()
     loads = [
         pltpu.make_async_copy(source, target, load_sem.at[i])
@@ -718,7 +729,7 @@
         + [(yes, place(axis, step)[1]) for axis in size for step in range(1, size[axis])],
         meanwhile,
     )
-    halo = Halo(spot, frame, buffers[12], *sems[0:6])
+    halo = Halo(spot, frame, held[0:3], *sems[0:9])
     halo.begin(0)
     halo.begin(1)
     halo.aside()
@@ -740,11 +751,11 @@
     halo.end()
     common = (left, right, accum, grad, scale, padded, patch, fields, halves)
     work(0, order, offsets, frame, probe_re, probe_im, amps, loads[4].wait, *common)
-    fold = Fold(spot, accum, *buffers[0:6], *sems[6:12])
-    halo = Halo(spot, frame, buffers[13], *sems[12:18])
+    fold = Fold(spot, accum, *buffers[0:5], held[3:6], *sems[9:18])
+    halo = Halo(spot, frame, held[6:9], *sems[18:27])
     renew(spot, fold, halo, accum, frame, lambda ch: place_terms(ch, 0, order, offsets, accum, padded))
     work(1, order, offsets, frame, probe_re, probe_im, amps, lambda: None, *common)
-    fold = Fold(spot, accum, *buffers[6:12], *sems[18:24])
+    fold = Fold(spot, accum, *buffers[5:10], held[9:12], *sems[27:36])
     finish_all(fold, lambda ch: place_terms(ch, 1, order, offsets, accum, padded), accum, frame, grad, probe_re, probe_im, out_re, out_im, out, *rest)
 
 
@@ -776,7 +787,7 @@
         ]
         + fold_buffers()
         + fold_buffers()
-        + [held_buffer(), held_buffer()]
+        + held_buffers() * 4
         + exchange_sems() * 4
         + [
             pltpu.VMEM((512, F), f32),

time: 123 us -> 126 us (1.024)
  Pallas kernels: 123 us -> 125 us
    pallas_call x1, Pallas kernels: 120 us -> 122 us  [local(): pl.pallas_call(whole_kernel, out_shape=[tile_shape, tile_shape, jax.Shape...]
where the time goes in v5:
time: 126 us; the launch traced here: 125 us
  Pallas kernels  125 us (99%)
    pallas_call x1, Pallas kernels, local(): pl.pallas_call(whole_kernel, out_shape=[tile_shape, tile_shape, jax.Shape...  122 us

profile of v5, /device:TPU:1, one launch (start us, length us, event | category | flops | bytes accessed | tf_op | source)
XLA Modules:
  0.0 125.4 jit_solution(12437826318176743399)
XLA Ops:
  0.6 122.4 %shard_map.120 = (f32[256,256]{1,0:T(8,128)}, f32[256,256]{1,0:T(8,128)}, f32[1024,256]{1,0:T(8,128)}) custom-call(s32[1,1,8]{2,1,0:T(1,128)} %order.1, s32[1,1,2,8]{3,2,1,0:T(2,128)} %bitcast.3, f32[256,256]{1,0:T(8,128)} %re_ref.1, f32[256,256]{1,0:T(8,128)} %im_ref.1, f32[2,256,256]{2,1,0:T(8,128)} %probe_re_in.1, f32[2,256,256]{2,1,0:T(8,128)} %probe_im_in.1, ...), custom_call_target="tpu_custom_call" | custom-call | tf_op jit(solution)/shard_map/pallas_call | solution.py:767
  123.0 2.2 %shard_map.121 = (f32[256,256]{1,0:T(8,128)}, f32[256,256]{1,0:T(8,128)}, f32[2,256,256]{2,1,0:T(8,128)}, f32[2,256,256]{2,1,0:T(8,128)}) custom-call(f32[256,256]{1,0:T(8,128)} %get-tuple-element.7.a, f32[256,256]{1,0:T(8,128)} %get-tuple-element.8.b, f32[1024,256]{1,0:T(8,128)} %get-tuple-element.9.flat), custom_call_target="tpu_custom_call" | custom-call | tf_op jit(solution)/shard_map/pallas_call | solution.py:825
